TPU v7x, 8 devices: a whole 2x2x1 slice. The times are simulated.
8 devices in a mesh: data: 2 (over z, y), ctx: 4 (over x, core).
Axes of the slice: x: 2, y: 2, z: 1, core: 2. Of those that a mesh axis runs over, the one named last changes fastest.
Arguments:
- hidden: bfloat16 [256, 3584], P(('data', 'ctx')), parts along dimension 0
- seq_lens: int32 [256], P(('data', 'ctx')), parts along dimension 0
- w_query: bfloat16 [16, 3584, 3584], replicated
- w_key: bfloat16 [16, 3584, 512], replicated
- w_value: bfloat16 [16, 3584, 512], replicated
- w_out: bfloat16 [16, 3584, 3584], replicated
- k_prefix: bfloat16 [16, 1024, 4, 128], P(None, ('data', 'ctx')), parts along dimension 1
- v_prefix: bfloat16 [16, 1024, 4, 128], P(None, ('data', 'ctx')), parts along dimension 1
- k_suffix: bfloat16 [16, 256, 32, 4, 128], P(None, ('data', 'ctx')), parts along dimension 1
- v_suffix: bfloat16 [16, 256, 32, 4, 128], P(None, ('data', 'ctx')), parts along dimension 1
Outputs:
- output 1: bfloat16 [256, 3584], P(('data', 'ctx')), parts along dimension 0
- output 2: bfloat16 [16, 256, 32, 4, 128], P(None, ('data', 'ctx')), parts along dimension 1
- output 3: bfloat16 [16, 256, 32, 4, 128], P(None, ('data', 'ctx')), parts along dimension 1
There are 2 independent parts. A program takes and returns all parts, laid end to end along the dimension named above; an argument that names none is the same for every part.
All inputs are finite; a program needn't handle non-finite values.
Results may differ from a plain program's by a relative error of at most 0.02.
Values are sent between devices in bfloat16 or wider.
A program may use at most 4 GiB of HBM per device.

v0:
```python
import jax
import jax.numpy as jnp
from jax import lax
from jax.sharding import PartitionSpec as P


def solution(mesh):
    ctx_size = mesh.shape['ctx']
    home_axes = ('data', 'ctx')
    row_spec = P(home_axes, None)
    lens_spec = P(home_axes)
    whole_spec = P()
    prefix_spec = P(None, home_axes, None, None)
    cache_spec = P(None, home_axes, None, None, None)

    def local_step(hidden, seq_lens, w_query, w_key, w_value, w_out, k_prefix, v_prefix, k_suffix, v_suffix):
        layers = w_query.shape[0]
        kv_heads = k_prefix.shape[2]
        head_dim = k_prefix.shape[3]
        num_heads = w_query.shape[2] // head_dim
        group_size = num_heads // kv_heads
        home_rows = hidden.shape[0]
        slot_count = k_suffix.shape[2]
        score_scale = head_dim ** -0.5
        slot_ids = lax.broadcasted_iota(jnp.int32, (home_rows, slot_count), 1)
        slot_hit = (slot_ids == seq_lens[:, None])[:, :, None, None]
        slot_live = (slot_ids <= seq_lens[:, None])[:, None, None, :]
        k_layers = []
        v_layers = []
        for layer_idx in range(layers):
            queries = jnp.dot(hidden, w_query[layer_idx], preferred_element_type=jnp.float32).astype(jnp.bfloat16).reshape(home_rows, kv_heads, group_size, head_dim)
            k_new = jnp.dot(hidden, w_key[layer_idx], preferred_element_type=jnp.float32).astype(jnp.bfloat16).reshape(home_rows, 1, kv_heads, head_dim)
            v_new = jnp.dot(hidden, w_value[layer_idx], preferred_element_type=jnp.float32).astype(jnp.bfloat16).reshape(home_rows, 1, kv_heads, head_dim)
            k_cache = jnp.where(slot_hit, k_new, k_suffix[layer_idx])
            v_cache = jnp.where(slot_hit, v_new, v_suffix[layer_idx])
            k_layers.append(k_cache)
            v_layers.append(v_cache)
            group_queries = lax.all_gather(queries, 'ctx', axis=0, tiled=True)
            pre_scores = jnp.einsum('bkgd,pkd->bkgp', group_queries, k_prefix[layer_idx], preferred_element_type=jnp.float32) * score_scale
            pre_max = pre_scores.max(axis=-1)
            pre_exp = jnp.exp(pre_scores - pre_max[..., None])
            pre_mass = pre_exp.sum(axis=-1)
            pre_vals = jnp.einsum('bkgp,pkd->bkgd', pre_exp.astype(jnp.bfloat16), v_prefix[layer_idx], preferred_element_type=jnp.float32)
            part_out = (pre_vals / pre_mass[..., None]).astype(jnp.bfloat16)
            part_lse = pre_max + jnp.log(pre_mass)
            home_out = lax.all_to_all(part_out, 'ctx', 0, 0, tiled=True).reshape(ctx_size, home_rows, kv_heads, group_size, head_dim)
            home_lse = lax.all_to_all(part_lse, 'ctx', 0, 0, tiled=True).reshape(ctx_size, home_rows, kv_heads, group_size)
            suf_scores = jnp.einsum('bkgd,bskd->bkgs', queries, k_cache, preferred_element_type=jnp.float32) * score_scale
            suf_scores = jnp.where(slot_live, suf_scores, -jnp.inf)
            suf_max = suf_scores.max(axis=-1)
            suf_exp = jnp.exp(suf_scores - suf_max[..., None])
            suf_mass = suf_exp.sum(axis=-1)
            suf_vals = jnp.einsum('bkgs,bskd->bkgd', suf_exp.astype(jnp.bfloat16), v_cache, preferred_element_type=jnp.float32)
            row_max = jnp.maximum(home_lse.max(axis=0), suf_max)
            part_weight = jnp.exp(home_lse - row_max)
            suf_weight = jnp.exp(suf_max - row_max)
            mass_sum = part_weight.sum(axis=0) + suf_weight * suf_mass
            mixed_sum = (part_weight[..., None] * home_out.astype(jnp.float32)).sum(axis=0) + suf_weight[..., None] * suf_vals
            attended = (mixed_sum / mass_sum[..., None]).astype(jnp.bfloat16).reshape(home_rows, num_heads * head_dim)
            update = jnp.dot(attended, w_out[layer_idx], preferred_element_type=jnp.float32).astype(jnp.bfloat16)
            hidden = (hidden.astype(jnp.float32) + update.astype(jnp.float32)).astype(jnp.bfloat16)
        return hidden, jnp.stack(k_layers), jnp.stack(v_layers)

    return jax.shard_map(local_step, mesh=mesh, in_specs=(row_spec, lens_spec, whole_spec, whole_spec, whole_spec, whole_spec, prefix_spec, prefix_spec, cache_spec, cache_spec), out_specs=(row_spec, cache_spec, cache_spec), check_vma=False)
```

profile of v0, /device:TPU:0, one launch (start us, length us, event | category | flops | bytes accessed | tf_op | source)
XLA Modules:
  0.0 1212.8 jit_solution(15157939997699789197)
XLA Ops:
  0.6 10.8 fusion.96
  11.9 14.3 %all_gather.48 = bf16[128,4,7,128]{3,0,2,1:T(8,128)(2,1)S(1)} all-gather(bf16[32,4,7,128]{3,0,2,1:T(8,128)(2,1)S(1)} %copy.525), channel_id=1, replica_groups=mesh['data'=2,'ctx'=4] {'ctx'}, dimensions={0}, use_global_device_ids=true | all-gather | bytes 1146880 | tf_op jit(solution)/shard_map/all_gather | solution.py:38
  60.3 6.6 all-to-all-done.1
  68.6 10.7 fusion.108
  85.0 10.6 fusion.111
  96.1 12.4 %all_gather.49 = bf16[128,4,7,128]{3,0,2,1:T(8,128)(2,1)S(1)} all-gather(bf16[32,4,7,128]{3,0,2,1:T(8,128)(2,1)S(1)} %copy.542), channel_id=1, replica_groups=mesh['data'=2,'ctx'=4] {'ctx'}, dimensions={0}, use_global_device_ids=true | all-gather | bytes 1146880 | tf_op jit(solution)/shard_map/all_gather | solution.py:38
  131.2 7.1 all-to-all-done.3
  140.1 10.7 fusion.123
  156.3 10.7 fusion.126
  167.4 12.4 %all_gather.50 = bf16[128,4,7,128]{3,0,2,1:T(8,128)(2,1)S(1)} all-gather(bf16[32,4,7,128]{3,0,2,1:T(8,128)(2,1)S(1)} %copy.559), channel_id=1, replica_groups=mesh['data'=2,'ctx'=4] {'ctx'}, dimensions={0}, use_global_device_ids=true | all-gather | bytes 1146880 | tf_op jit(solution)/shard_map/all_gather | solution.py:38
  202.6 7.1 all-to-all-done.5
  211.4 10.7 fusion.138
  227.7 10.6 fusion.141
  238.9 12.4 %all_gather.51 = bf16[128,4,7,128]{3,0,2,1:T(8,128)(2,1)S(1)} all-gather(bf16[32,4,7,128]{3,0,2,1:T(8,128)(2,1)S(1)} %copy.576), channel_id=1, replica_groups=mesh['data'=2,'ctx'=4] {'ctx'}, dimensions={0}, use_global_device_ids=true | all-gather | bytes 1146880 | tf_op jit(solution)/shard_map/all_gather | solution.py:38
  274.2 7.1 all-to-all-done.7
  283.1 10.7 fusion.153
  299.3 10.7 fusion.156
  310.4 12.4 %all_gather.52 = bf16[128,4,7,128]{3,0,2,1:T(8,128)(2,1)S(1)} all-gather(bf16[32,4,7,128]{3,0,2,1:T(8,128)(2,1)S(1)} %copy.593), channel_id=1, replica_groups=mesh['data'=2,'ctx'=4] {'ctx'}, dimensions={0}, use_global_device_ids=true | all-gather | bytes 1146880 | tf_op jit(solution)/shard_map/all_gather | solution.py:38
  345.6 7.1 all-to-all-done.9
  354.4 10.7 fusion.168
  370.7 10.7 fusion.171
  381.9 12.4 %all_gather.53 = bf16[128,4,7,128]{3,0,2,1:T(8,128)(2,1)S(1)} all-gather(bf16[32,4,7,128]{3,0,2,1:T(8,128)(2,1)S(1)} %copy.610), channel_id=1, replica_groups=mesh['data'=2,'ctx'=4] {'ctx'}, dimensions={0}, use_global_device_ids=true | all-gather | bytes 1146880 | tf_op jit(solution)/shard_map/all_gather | solution.py:38
  417.1 7.1 all-to-all-done.11
  425.9 10.7 fusion.183
  442.1 10.7 fusion.186
  453.3 12.4 %all_gather.54 = bf16[128,4,7,128]{3,0,2,1:T(8,128)(2,1)S(1)} all-gather(bf16[32,4,7,128]{3,0,2,1:T(8,128)(2,1)S(1)} %copy.627), channel_id=1, replica_groups=mesh['data'=2,'ctx'=4] {'ctx'}, dimensions={0}, use_global_device_ids=true | all-gather | bytes 1146880 | tf_op jit(solution)/shard_map/all_gather | solution.py:38
  488.7 7.1 all-to-all-done.13
  497.5 10.7 fusion.198
  513.8 10.7 fusion.201
  525.0 12.4 %all_gather.55 = bf16[128,4,7,128]{3,0,2,1:T(8,128)(2,1)S(1)} all-gather(bf16[32,4,7,128]{3,0,2,1:T(8,128)(2,1)S(1)} %copy.644), channel_id=1, replica_groups=mesh['data'=2,'ctx'=4] {'ctx'}, dimensions={0}, use_global_device_ids=true | all-gather | bytes 1146880 | tf_op jit(solution)/shard_map/all_gather | solution.py:38
  560.2 7.1 all-to-all-done.15
  569.0 10.7 fusion.213
  585.2 10.8 fusion.216
  596.5 12.4 %all_gather.56 = bf16[128,4,7,128]{3,0,2,1:T(8,128)(2,1)S(1)} all-gather(bf16[32,4,7,128]{3,0,2,1:T(8,128)(2,1)S(1)} %copy.661), channel_id=1, replica_groups=mesh['data'=2,'ctx'=4] {'ctx'}, dimensions={0}, use_global_device_ids=true | all-gather | bytes 1146880 | tf_op jit(solution)/shard_map/all_gather | solution.py:38
  631.7 7.1 all-to-all-done.17
  640.5 10.7 fusion.228
  656.9 10.7 fusion.231
  668.0 12.4 %all_gather.57 = bf16[128,4,7,128]{3,0,2,1:T(8,128)(2,1)S(1)} all-gather(bf16[32,4,7,128]{3,0,2,1:T(8,128)(2,1)S(1)} %copy.678), channel_id=1, replica_groups=mesh['data'=2,'ctx'=4] {'ctx'}, dimensions={0}, use_global_device_ids=true | all-gather | bytes 1146880 | tf_op jit(solution)/shard_map/all_gather | solution.py:38
  703.4 7.1 all-to-all-done.19
  712.3 10.7 fusion.243
  728.5 10.7 fusion.246
  739.6 12.4 %all_gather.58 = bf16[128,4,7,128]{3,0,2,1:T(8,128)(2,1)S(1)} all-gather(bf16[32,4,7,128]{3,0,2,1:T(8,128)(2,1)S(1)} %copy.695), channel_id=1, replica_groups=mesh['data'=2,'ctx'=4] {'ctx'}, dimensions={0}, use_global_device_ids=true | all-gather | bytes 1146880 | tf_op jit(solution)/shard_map/all_gather | solution.py:38
  774.8 7.1 all-to-all-done.21
  783.6 10.7 fusion.258
  799.9 10.8 fusion.261
  811.2 12.4 %all_gather.59 = bf16[128,4,7,128]{3,0,2,1:T(8,128)(2,1)S(1)} all-gather(bf16[32,4,7,128]{3,0,2,1:T(8,128)(2,1)S(1)} %copy.712), channel_id=1, replica_groups=mesh['data'=2,'ctx'=4] {'ctx'}, dimensions={0}, use_global_device_ids=true | all-gather | bytes 1146880 | tf_op jit(solution)/shard_map/all_gather | solution.py:38
  846.4 7.1 all-to-all-done.23
  855.2 10.7 fusion.273
  871.4 10.7 fusion.276
  882.6 12.4 %all_gather.60 = bf16[128,4,7,128]{3,0,2,1:T(8,128)(2,1)S(1)} all-gather(bf16[32,4,7,128]{3,0,2,1:T(8,128)(2,1)S(1)} %copy.729), channel_id=1, replica_groups=mesh['data'=2,'ctx'=4] {'ctx'}, dimensions={0}, use_global_device_ids=true | all-gather | bytes 1146880 | tf_op jit(solution)/shard_map/all_gather | solution.py:38
  918.0 7.1 all-to-all-done.25
  926.8 10.7 fusion.288
  943.1 10.7 fusion.291
  954.3 12.4 %all_gather.61 = bf16[128,4,7,128]{3,0,2,1:T(8,128)(2,1)S(1)} all-gather(bf16[32,4,7,128]{3,0,2,1:T(8,128)(2,1)S(1)} %copy.746), channel_id=1, replica_groups=mesh['data'=2,'ctx'=4] {'ctx'}, dimensions={0}, use_global_device_ids=true | all-gather | bytes 1146880 | tf_op jit(solution)/shard_map/all_gather | solution.py:38
  989.4 7.1 all-to-all-done.27
  998.3 10.7 fusion.303
  1014.6 10.7 fusion.306
  1025.7 12.4 %all_gather.62 = bf16[128,4,7,128]{3,0,2,1:T(8,128)(2,1)S(1)} all-gather(bf16[32,4,7,128]{3,0,2,1:T(8,128)(2,1)S(1)} %copy.763), channel_id=1, replica_groups=mesh['data'=2,'ctx'=4] {'ctx'}, dimensions={0}, use_global_device_ids=true | all-gather | bytes 1146880 | tf_op jit(solution)/shard_map/all_gather | solution.py:38
  1061.5 9.7 all-to-all-done.29
  1072.9 10.7 fusion.318
  1089.1 10.7 fusion.321
  1100.3 12.4 %all_gather.63 = bf16[128,4,7,128]{3,0,2,1:T(8,128)(2,1)S(1)} all-gather(bf16[32,4,7,128]{3,0,2,1:T(8,128)(2,1)S(1)} %copy.780), channel_id=1, replica_groups=mesh['data'=2,'ctx'=4] {'ctx'}, dimensions={0}, use_global_device_ids=true | all-gather | bytes 1146880 | tf_op jit(solution)/shard_map/all_gather | solution.py:38
  1192.2 7.1 all-to-all-done.31
  1201.0 11.3 fusion.333
  (766 shorter events, 549.5 us)
Async XLA Ops:
  0.6 25.5 %copy-start = (bf16[16,128,4,128]{3,2,1,0:T(4,128)(2,1)S(1)}, bf16[16,128,4,128]{3,2,1,0:T(4,128)(2,1)}, u32[]{:S(2)}) copy-start(bf16[16,128,4,128]{3,2,1,0:T(4,128)(2,1)} %param.16) | copy-start | bytes 6291460
  29.7 20.4 %all-to-all-start = ((f32[4,1,896]{2,1,0:T(1,128)}), f32[4,1,896]{2,1,0:T(1,128)S(1)}, u32[]{:S(2)}, u32[]{:S(2)}) async-start(f32[4,1,896]{2,1,0:T(1,128)} %reshape.886), calls=%async_computation | async-start | bytes 28672 | tf_op jit(solution)/shard_map/all_to_all | solution.py:47
  50.2 16.7 %all-to-all-start.1 = ((bf16[128,4,7,128]{3,1,2,0:T(4,128)(2,1)}), bf16[128,4,7,128]{3,1,2,0:T(4,128)(2,1)S(1)}, u32[]{:S(2)}, u32[]{:S(2)}) async-start(bf16[128,4,7,128]{3,1,2,0:T(4,128)(2,1)} %copy.534), calls=%async_computation.1 | async-start | bytes 1835008 | tf_op jit(solution)/shard_map/all_to_all | solution.py:46
  95.6 13.7 %copy-start.66 = (bf16[1,128,4,128]{3,2,1,0:T(4,128)(2,1)S(1)}, bf16[1,128,4,128]{3,2,1,0:T(4,128)(2,1)}, u32[]{:S(2)}) copy-start(bf16[1,128,4,128]{3,2,1,0:T(4,128)(2,1)} %get-tuple-element.81) | copy-start | bytes 393220
  95.7 19.9 %copy-start.28 = (bf16[32,4,128]{2,1,0:T(4,128)(2,1)}, bf16[32,4,128]{2,1,0:T(4,128)(2,1)S(1)}, u32[]{:S(2)}) copy-start(bf16[32,4,128]{2,1,0:T(4,128)(2,1)S(1)} %broadcast_in_dim.589) | copy-start | bytes 98308
  112.2 9.7 all-to-all-start.2
  121.9 16.5 %all-to-all-start.3 = ((bf16[128,4,7,128]{3,1,2,0:T(4,128)(2,1)}), bf16[128,4,7,128]{3,1,2,0:T(4,128)(2,1)S(1)}, u32[]{:S(2)}, u32[]{:S(2)}) async-start(bf16[128,4,7,128]{3,1,2,0:T(4,128)(2,1)} %copy.551), calls=%async_computation.3 | async-start | bytes 1835008 | tf_op jit(solution)/shard_map/all_to_all | solution.py:46
  166.9 13.8 %copy-start.65 = (bf16[1,128,4,128]{3,2,1,0:T(4,128)(2,1)S(1)}, bf16[1,128,4,128]{3,2,1,0:T(4,128)(2,1)}, u32[]{:S(2)}) copy-start(bf16[1,128,4,128]{3,2,1,0:T(4,128)(2,1)} %get-tuple-element.80) | copy-start | bytes 393220
  167.0 19.9 %copy-start.32 = (bf16[32,4,128]{2,1,0:T(4,128)(2,1)}, bf16[32,4,128]{2,1,0:T(4,128)(2,1)S(1)}, u32[]{:S(2)}) copy-start(bf16[32,4,128]{2,1,0:T(4,128)(2,1)S(1)} %broadcast_in_dim.593) | copy-start | bytes 98308
  183.5 9.7 all-to-all-start.4
  193.2 16.5 %all-to-all-start.5 = ((bf16[128,4,7,128]{3,1,2,0:T(4,128)(2,1)}), bf16[128,4,7,128]{3,1,2,0:T(4,128)(2,1)S(1)}, u32[]{:S(2)}, u32[]{:S(2)}) async-start(bf16[128,4,7,128]{3,1,2,0:T(4,128)(2,1)} %copy.568), calls=%async_computation.5 | async-start | bytes 1835008 | tf_op jit(solution)/shard_map/all_to_all | solution.py:46
  238.4 19.9 %copy-start.34 = (bf16[32,4,128]{2,1,0:T(4,128)(2,1)}, bf16[32,4,128]{2,1,0:T(4,128)(2,1)S(1)}, u32[]{:S(2)}) copy-start(bf16[32,4,128]{2,1,0:T(4,128)(2,1)S(1)} %broadcast_in_dim.597) | copy-start | bytes 98308
  255.0 9.7 all-to-all-start.6
  264.7 16.7 %all-to-all-start.7 = ((bf16[128,4,7,128]{3,1,2,0:T(4,128)(2,1)}), bf16[128,4,7,128]{3,1,2,0:T(4,128)(2,1)S(1)}, u32[]{:S(2)}, u32[]{:S(2)}) async-start(bf16[128,4,7,128]{3,1,2,0:T(4,128)(2,1)} %copy.585), calls=%async_computation.7 | async-start | bytes 1835008 | tf_op jit(solution)/shard_map/all_to_all | solution.py:46
  310.0 13.7 %copy-start.63 = (bf16[1,128,4,128]{3,2,1,0:T(4,128)(2,1)S(1)}, bf16[1,128,4,128]{3,2,1,0:T(4,128)(2,1)}, u32[]{:S(2)}) copy-start(bf16[1,128,4,128]{3,2,1,0:T(4,128)(2,1)} %get-tuple-element.78) | copy-start | bytes 393220
  310.0 19.9 %copy-start.36 = (bf16[32,4,128]{2,1,0:T(4,128)(2,1)}, bf16[32,4,128]{2,1,0:T(4,128)(2,1)S(1)}, u32[]{:S(2)}) copy-start(bf16[32,4,128]{2,1,0:T(4,128)(2,1)S(1)} %broadcast_in_dim.601) | copy-start | bytes 98308
  326.6 9.7 all-to-all-start.8
  336.2 16.5 %all-to-all-start.9 = ((bf16[128,4,7,128]{3,1,2,0:T(4,128)(2,1)}), bf16[128,4,7,128]{3,1,2,0:T(4,128)(2,1)S(1)}, u32[]{:S(2)}, u32[]{:S(2)}) async-start(bf16[128,4,7,128]{3,1,2,0:T(4,128)(2,1)} %copy.602), calls=%async_computation.9 | async-start | bytes 1835008 | tf_op jit(solution)/shard_map/all_to_all | solution.py:46
  370.7 23.6 %copy-start.27 = (bf16[1,128,4,128]{3,2,1,0:T(4,128)(2,1)S(1)}, bf16[1,128,4,128]{3,2,1,0:T(4,128)(2,1)}, u32[]{:S(2)}) copy-start(bf16[1,128,4,128]{3,2,1,0:T(4,128)(2,1)} %get-tuple-element.93) | copy-start | bytes 393220
  381.4 13.7 %copy-start.62 = (bf16[1,128,4,128]{3,2,1,0:T(4,128)(2,1)S(1)}, bf16[1,128,4,128]{3,2,1,0:T(4,128)(2,1)}, u32[]{:S(2)}) copy-start(bf16[1,128,4,128]{3,2,1,0:T(4,128)(2,1)} %get-tuple-element.77) | copy-start | bytes 393220
  381.5 19.9 %copy-start.38 = (bf16[32,4,128]{2,1,0:T(4,128)(2,1)}, bf16[32,4,128]{2,1,0:T(4,128)(2,1)S(1)}, u32[]{:S(2)}) copy-start(bf16[32,4,128]{2,1,0:T(4,128)(2,1)S(1)} %broadcast_in_dim.605) | copy-start | bytes 98308
  398.0 9.7 all-to-all-start.10
  407.7 16.5 %all-to-all-start.11 = ((bf16[128,4,7,128]{3,1,2,0:T(4,128)(2,1)}), bf16[128,4,7,128]{3,1,2,0:T(4,128)(2,1)S(1)}, u32[]{:S(2)}, u32[]{:S(2)}) async-start(bf16[128,4,7,128]{3,1,2,0:T(4,128)(2,1)} %copy.619), calls=%async_computation.11 | async-start | bytes 1835008 | tf_op jit(solution)/shard_map/all_to_all | solution.py:46
  442.1 23.6 %copy-start.26 = (bf16[1,128,4,128]{3,2,1,0:T(4,128)(2,1)S(1)}, bf16[1,128,4,128]{3,2,1,0:T(4,128)(2,1)}, u32[]{:S(2)}) copy-start(bf16[1,128,4,128]{3,2,1,0:T(4,128)(2,1)} %get-tuple-element.92) | copy-start | bytes 393220
  452.8 13.7 %copy-start.61 = (bf16[1,128,4,128]{3,2,1,0:T(4,128)(2,1)S(1)}, bf16[1,128,4,128]{3,2,1,0:T(4,128)(2,1)}, u32[]{:S(2)}) copy-start(bf16[1,128,4,128]{3,2,1,0:T(4,128)(2,1)} %get-tuple-element.76) | copy-start | bytes 393220
  452.9 19.9 %copy-start.40 = (bf16[32,4,128]{2,1,0:T(4,128)(2,1)}, bf16[32,4,128]{2,1,0:T(4,128)(2,1)S(1)}, u32[]{:S(2)}) copy-start(bf16[32,4,128]{2,1,0:T(4,128)(2,1)S(1)} %broadcast_in_dim.609) | copy-start | bytes 98308
  469.4 9.7 all-to-all-start.12
  479.1 16.7 %all-to-all-start.13 = ((bf16[128,4,7,128]{3,1,2,0:T(4,128)(2,1)}), bf16[128,4,7,128]{3,1,2,0:T(4,128)(2,1)S(1)}, u32[]{:S(2)}, u32[]{:S(2)}) async-start(bf16[128,4,7,128]{3,1,2,0:T(4,128)(2,1)} %copy.636), calls=%async_computation.13 | async-start | bytes 1835008 | tf_op jit(solution)/shard_map/all_to_all | solution.py:46
  513.8 23.6 %copy-start.25 = (bf16[1,128,4,128]{3,2,1,0:T(4,128)(2,1)S(1)}, bf16[1,128,4,128]{3,2,1,0:T(4,128)(2,1)}, u32[]{:S(2)}) copy-start(bf16[1,128,4,128]{3,2,1,0:T(4,128)(2,1)} %get-tuple-element.91) | copy-start | bytes 393220
  524.6 19.9 %copy-start.42 = (bf16[32,4,128]{2,1,0:T(4,128)(2,1)}, bf16[32,4,128]{2,1,0:T(4,128)(2,1)S(1)}, u32[]{:S(2)}) copy-start(bf16[32,4,128]{2,1,0:T(4,128)(2,1)S(1)} %broadcast_in_dim.613) | copy-start | bytes 98308
  541.1 9.7 all-to-all-start.14
  550.8 16.5 %all-to-all-start.15 = ((bf16[128,4,7,128]{3,1,2,0:T(4,128)(2,1)}), bf16[128,4,7,128]{3,1,2,0:T(4,128)(2,1)S(1)}, u32[]{:S(2)}, u32[]{:S(2)}) async-start(bf16[128,4,7,128]{3,1,2,0:T(4,128)(2,1)} %copy.653), calls=%async_computation.15 | async-start | bytes 1835008 | tf_op jit(solution)/shard_map/all_to_all | solution.py:46
  585.2 23.8 %copy-start.24 = (bf16[1,128,4,128]{3,2,1,0:T(4,128)(2,1)S(1)}, bf16[1,128,4,128]{3,2,1,0:T(4,128)(2,1)}, u32[]{:S(2)}) copy-start(bf16[1,128,4,128]{3,2,1,0:T(4,128)(2,1)} %get-tuple-element.90) | copy-start | bytes 393220
  596.0 13.7 %copy-start.59 = (bf16[1,128,4,128]{3,2,1,0:T(4,128)(2,1)S(1)}, bf16[1,128,4,128]{3,2,1,0:T(4,128)(2,1)}, u32[]{:S(2)}) copy-start(bf16[1,128,4,128]{3,2,1,0:T(4,128)(2,1)} %get-tuple-element.74) | copy-start | bytes 393220
  596.1 19.9 %copy-start.44 = (bf16[32,4,128]{2,1,0:T(4,128)(2,1)}, bf16[32,4,128]{2,1,0:T(4,128)(2,1)S(1)}, u32[]{:S(2)}) copy-start(bf16[32,4,128]{2,1,0:T(4,128)(2,1)S(1)} %broadcast_in_dim.617) | copy-start | bytes 98308
  612.6 9.7 all-to-all-start.16
  622.3 16.5 %all-to-all-start.17 = ((bf16[128,4,7,128]{3,1,2,0:T(4,128)(2,1)}), bf16[128,4,7,128]{3,1,2,0:T(4,128)(2,1)S(1)}, u32[]{:S(2)}, u32[]{:S(2)}) async-start(bf16[128,4,7,128]{3,1,2,0:T(4,128)(2,1)} %copy.670), calls=%async_computation.17 | async-start | bytes 1835008 | tf_op jit(solution)/shard_map/all_to_all | solution.py:46
  656.8 23.6 %copy-start.23 = (bf16[1,128,4,128]{3,2,1,0:T(4,128)(2,1)S(1)}, bf16[1,128,4,128]{3,2,1,0:T(4,128)(2,1)}, u32[]{:S(2)}) copy-start(bf16[1,128,4,128]{3,2,1,0:T(4,128)(2,1)} %get-tuple-element.89) | copy-start | bytes 393220
  667.5 13.7 %copy-start.58 = (bf16[1,128,4,128]{3,2,1,0:T(4,128)(2,1)S(1)}, bf16[1,128,4,128]{3,2,1,0:T(4,128)(2,1)}, u32[]{:S(2)}) copy-start(bf16[1,128,4,128]{3,2,1,0:T(4,128)(2,1)} %get-tuple-element.73) | copy-start | bytes 393220
  667.6 19.9 %copy-start.46 = (bf16[32,4,128]{2,1,0:T(4,128)(2,1)}, bf16[32,4,128]{2,1,0:T(4,128)(2,1)S(1)}, u32[]{:S(2)}) copy-start(bf16[32,4,128]{2,1,0:T(4,128)(2,1)S(1)} %broadcast_in_dim.621) | copy-start | bytes 98308
  684.1 9.7 all-to-all-start.18
  693.8 16.7 %all-to-all-start.19 = ((bf16[128,4,7,128]{3,1,2,0:T(4,128)(2,1)}), bf16[128,4,7,128]{3,1,2,0:T(4,128)(2,1)S(1)}, u32[]{:S(2)}, u32[]{:S(2)}) async-start(bf16[128,4,7,128]{3,1,2,0:T(4,128)(2,1)} %copy.687), calls=%async_computation.19 | async-start | bytes 1835008 | tf_op jit(solution)/shard_map/all_to_all | solution.py:46
  728.5 23.6 %copy-start.22 = (bf16[1,128,4,128]{3,2,1,0:T(4,128)(2,1)S(1)}, bf16[1,128,4,128]{3,2,1,0:T(4,128)(2,1)}, u32[]{:S(2)}) copy-start(bf16[1,128,4,128]{3,2,1,0:T(4,128)(2,1)} %get-tuple-element.88) | copy-start | bytes 393220
  739.2 13.7 %copy-start.57 = (bf16[1,128,4,128]{3,2,1,0:T(4,128)(2,1)S(1)}, bf16[1,128,4,128]{3,2,1,0:T(4,128)(2,1)}, u32[]{:S(2)}) copy-start(bf16[1,128,4,128]{3,2,1,0:T(4,128)(2,1)} %get-tuple-element.72) | copy-start | bytes 393220
  739.2 19.9 %copy-start.48 = (bf16[32,4,128]{2,1,0:T(4,128)(2,1)}, bf16[32,4,128]{2,1,0:T(4,128)(2,1)S(1)}, u32[]{:S(2)}) copy-start(bf16[32,4,128]{2,1,0:T(4,128)(2,1)S(1)} %broadcast_in_dim.625) | copy-start | bytes 98308
  755.8 9.7 all-to-all-start.20
  765.4 16.5 %all-to-all-start.21 = ((bf16[128,4,7,128]{3,1,2,0:T(4,128)(2,1)}), bf16[128,4,7,128]{3,1,2,0:T(4,128)(2,1)S(1)}, u32[]{:S(2)}, u32[]{:S(2)}) async-start(bf16[128,4,7,128]{3,1,2,0:T(4,128)(2,1)} %copy.704), calls=%async_computation.21 | async-start | bytes 1835008 | tf_op jit(solution)/shard_map/all_to_all | solution.py:46
  799.9 23.7 %copy-start.21 = (bf16[1,128,4,128]{3,2,1,0:T(4,128)(2,1)S(1)}, bf16[1,128,4,128]{3,2,1,0:T(4,128)(2,1)}, u32[]{:S(2)}) copy-start(bf16[1,128,4,128]{3,2,1,0:T(4,128)(2,1)} %get-tuple-element.87) | copy-start | bytes 393220
  810.7 13.7 %copy-start.56 = (bf16[1,128,4,128]{3,2,1,0:T(4,128)(2,1)S(1)}, bf16[1,128,4,128]{3,2,1,0:T(4,128)(2,1)}, u32[]{:S(2)}) copy-start(bf16[1,128,4,128]{3,2,1,0:T(4,128)(2,1)} %get-tuple-element.71) | copy-start | bytes 393220
  810.8 19.9 %copy-start.50 = (bf16[32,4,128]{2,1,0:T(4,128)(2,1)}, bf16[32,4,128]{2,1,0:T(4,128)(2,1)S(1)}, u32[]{:S(2)}) copy-start(bf16[32,4,128]{2,1,0:T(4,128)(2,1)S(1)} %broadcast_in_dim.629) | copy-start | bytes 98308
  827.3 9.7 all-to-all-start.22
  837.0 16.5 %all-to-all-start.23 = ((bf16[128,4,7,128]{3,1,2,0:T(4,128)(2,1)}), bf16[128,4,7,128]{3,1,2,0:T(4,128)(2,1)S(1)}, u32[]{:S(2)}, u32[]{:S(2)}) async-start(bf16[128,4,7,128]{3,1,2,0:T(4,128)(2,1)} %copy.721), calls=%async_computation.23 | async-start | bytes 1835008 | tf_op jit(solution)/shard_map/all_to_all | solution.py:46
  871.4 23.6 %copy-start.20 = (bf16[1,128,4,128]{3,2,1,0:T(4,128)(2,1)S(1)}, bf16[1,128,4,128]{3,2,1,0:T(4,128)(2,1)}, u32[]{:S(2)}) copy-start(bf16[1,128,4,128]{3,2,1,0:T(4,128)(2,1)} %get-tuple-element.86) | copy-start | bytes 393220
  898.7 9.7 all-to-all-start.24
  908.4 16.7 %all-to-all-start.25 = ((bf16[128,4,7,128]{3,1,2,0:T(4,128)(2,1)}), bf16[128,4,7,128]{3,1,2,0:T(4,128)(2,1)S(1)}, u32[]{:S(2)}, u32[]{:S(2)}) async-start(bf16[128,4,7,128]{3,1,2,0:T(4,128)(2,1)} %copy.738), calls=%async_computation.25 | async-start | bytes 1835008 | tf_op jit(solution)/shard_map/all_to_all | solution.py:46
  943.1 23.6 %copy-start.19 = (bf16[1,128,4,128]{3,2,1,0:T(4,128)(2,1)S(1)}, bf16[1,128,4,128]{3,2,1,0:T(4,128)(2,1)}, u32[]{:S(2)}) copy-start(bf16[1,128,4,128]{3,2,1,0:T(4,128)(2,1)} %get-tuple-element.85) | copy-start | bytes 393220
  970.4 9.7 all-to-all-start.26
  980.1 16.5 %all-to-all-start.27 = ((bf16[128,4,7,128]{3,1,2,0:T(4,128)(2,1)}), bf16[128,4,7,128]{3,1,2,0:T(4,128)(2,1)S(1)}, u32[]{:S(2)}, u32[]{:S(2)}) async-start(bf16[128,4,7,128]{3,1,2,0:T(4,128)(2,1)} %copy.755), calls=%async_computation.27 | async-start | bytes 1835008 | tf_op jit(solution)/shard_map/all_to_all | solution.py:46
  1014.6 23.6 %copy-start.18 = (bf16[1,128,4,128]{3,2,1,0:T(4,128)(2,1)S(1)}, bf16[1,128,4,128]{3,2,1,0:T(4,128)(2,1)}, u32[]{:S(2)}) copy-start(bf16[1,128,4,128]{3,2,1,0:T(4,128)(2,1)} %get-tuple-element.84) | copy-start | bytes 393220
  1040.1 14.6 %all-to-all-start.28 = ((f32[4,1,896]{2,1,0:T(1,128)}), f32[4,1,896]{2,1,0:T(1,128)S(1)}, u32[]{:S(2)}, u32[]{:S(2)}) async-start(f32[4,1,896]{2,1,0:T(1,128)} %reshape.914), calls=%async_computation.28 | async-start | bytes 28672 | tf_op jit(solution)/shard_map/all_to_all | solution.py:47
  1054.7 16.5 %all-to-all-start.29 = ((bf16[128,4,7,128]{3,1,2,0:T(4,128)(2,1)}), bf16[128,4,7,128]{3,1,2,0:T(4,128)(2,1)S(1)}, u32[]{:S(2)}, u32[]{:S(2)}) async-start(bf16[128,4,7,128]{3,1,2,0:T(4,128)(2,1)} %copy.772), calls=%async_computation.29 | async-start | bytes 1835008 | tf_op jit(solution)/shard_map/all_to_all | solution.py:46
  1089.1 23.6 %copy-start.17 = (bf16[1,128,4,128]{3,2,1,0:T(4,128)(2,1)S(1)}, bf16[1,128,4,128]{3,2,1,0:T(4,128)(2,1)}, u32[]{:S(2)}) copy-start(bf16[1,128,4,128]{3,2,1,0:T(4,128)(2,1)} %get-tuple-element.83) | copy-start | bytes 393220
  1116.4 66.5 %all-to-all-start.30 = ((f32[4,1,896]{2,1,0:T(1,128)}), f32[4,1,896]{2,1,0:T(1,128)S(1)}, u32[]{:S(2)}, u32[]{:S(2)}) async-start(f32[4,1,896]{2,1,0:T(1,128)} %reshape.916), calls=%async_computation.30 | async-start | bytes 28672 | tf_op jit(solution)/shard_map/all_to_all | solution.py:47
  1183.0 16.3 %all-to-all-start.31 = ((bf16[128,4,7,128]{3,1,2,0:T(4,128)(2,1)}), bf16[128,4,7,128]{3,1,2,0:T(4,128)(2,1)S(1)}, u32[]{:S(2)}, u32[]{:S(2)}) async-start(bf16[128,4,7,128]{3,1,2,0:T(4,128)(2,1)} %copy.789), calls=%async_computation.31 | async-start | bytes 1835008 | tf_op jit(solution)/shard_map/all_to_all | solution.py:46
  (54 other events, 407.8 us)
where the time goes:
time: 1230 us; the launch traced here: 1210 us
  matrix products  489 us (40%)
  other arithmetic  212 us (17%)
  blocking collectives  201 us (16%)
  waiting for transfers between devices  116 us (9%)
  starting transfers between devices  114 us (9%)
  local copies, waits for them, and re-layouts  77.3 us (6%)
    all_gather x16, blocking collectives, local_step(): group_queries = lax.all_gather(queries, 'ctx', axis=0, tiled=True)  201 us
    dot_general x16, matrix products, local_step(): jnp.dot(attended, w_out[layer_idx], preferred_element_type=jnp.float32)  171 us
    dot_general x16, matrix products, local_step(): jnp.dot(hidden, w_query[layer_idx], preferred_element_type=jnp.float32)  171 us
    all_to_all x16, waiting for transfers between devices, local_step(): lax.all_to_all(part_out, 'ctx', 0, 0, tiled=True)  116 us
    unnamed x28, other arithmetic  113 us
    all_to_all x16, starting transfers between devices, local_step(): lax.all_to_all(part_out, 'ctx', 0, 0, tiled=True)  60.3 us
    all_to_all x16, starting transfers between devices, local_step(): lax.all_to_all(part_lse, 'ctx', 0, 0, tiled=True)  53.9 us
    select_n x16, other arithmetic, local_step(): k_cache = jnp.where(slot_hit, k_new, k_suffix[layer_idx])  52.4 us
  transfers between devices with their start and end apart: 32, of which 16 were waited for; matrix products, arithmetic and copies ran while one was open for 22% of the time, Pallas kernels for 0%

commit v1 on v0

v1 whole, which is shorter than its diff:
```python
import functools

import jax
import jax.numpy as jnp
from jax import lax
from jax.experimental import pallas as pl
from jax.experimental.pallas import tpu as pltpu
from jax.sharding import PartitionSpec as P

MESH = pl.DeviceIdType.MESH
BF16 = jnp.bfloat16
F32 = jnp.float32
TILE = 512
CHUNK = 16
PAD = 8


def decode_kernel(dims, hidden_ref, lens_ref, wq_ref, wk_ref, wv_ref, wo_ref, pre_ref, ksuf_ref, vsuf_ref,
                  out_ref, kv_out_ref,
                  wq_buf, wk_buf, wv_buf, wo_buf, pre_buf, suf_buf, x_buf, own_buf, recv_buf, acc_buf, q_buf, kn_buf, vn_buf,
                  o_buf, att_buf, lens_buf, kv_send_buf,
                  w_sem, suf_load_sem, suf_send_sem, suf_recv_sem, pre_local_sem, pre_send_sem, pre_recv_sem,
                  part_send_sem, part_recv_sem, lens_sem, kv_sem):
    layers, rows, group, head_dim, slots = dims
    tiles = x_buf.shape[0]
    q_width = wq_buf.shape[2]
    kv_width = wk_buf.shape[2]
    both = 2 * rows
    me = lax.axis_index("ctx")
    core = lax.rem(me, 2)
    chip = me // 2
    mate = chip * 2 + (1 - core)
    across = (1 - chip) * 2 + core
    diagonal = (1 - chip) * 2 + (1 - core)
    peers = ((mate, 1 - core), (across, core), (diagonal, 1 - core))
    mine = pl.multiple_of(core * rows, rows)
    other = pl.multiple_of((1 - core) * rows, rows)
    q_col = pl.multiple_of(core * q_width, 128)
    kv_col = pl.multiple_of(core * kv_width, 128)
    scale = head_dim ** -0.5

    def qkv_copies(layer, j):
        r = pl.ds(pl.multiple_of(j * TILE, TILE), TILE)
        return (
            pltpu.make_async_copy(wq_ref.at[layer, r, pl.ds(q_col, q_width)], wq_buf.at[j], w_sem.at[0, j]),
            pltpu.make_async_copy(wk_ref.at[layer, r, pl.ds(kv_col, kv_width)], wk_buf.at[j], w_sem.at[1, j]),
            pltpu.make_async_copy(wv_ref.at[layer, r, pl.ds(kv_col, kv_width)], wv_buf.at[j], w_sem.at[2, j]),
        )

    def wo_copy(layer, j):
        cols = pl.ds(pl.multiple_of(j * TILE, TILE), TILE)
        return pltpu.make_async_copy(wo_ref.at[layer, pl.ds(q_col, q_width), cols], wo_buf.at[j], w_sem.at[3, j])

    def suf_loads(layer):
        slot = lax.rem(layer, 3)
        return (
            pltpu.make_async_copy(ksuf_ref.at[layer], suf_buf.at[slot, 0], suf_load_sem.at[slot, 0]),
            pltpu.make_async_copy(vsuf_ref.at[layer], suf_buf.at[slot, 1], suf_load_sem.at[slot, 1]),
        )

    def suf_send(layer):
        return pltpu.make_async_remote_copy(
            src_ref=suf_buf.at[lax.rem(layer, 3)], dst_ref=suf_buf.at[3 + lax.rem(layer, 2)],
            send_sem=suf_send_sem.at[lax.rem(layer, 2)], recv_sem=suf_recv_sem.at[lax.rem(layer, 2)],
            device_id={"ctx": mate}, device_id_type=MESH)

    def pre_local(layer):
        return pltpu.make_async_copy(pre_ref.at[layer, core], pre_buf.at[layer, :, :, me], pre_local_sem.at[layer])

    def pre_remote(layer, k):
        device, half = peers[k]
        return pltpu.make_async_remote_copy(
            src_ref=pre_ref.at[layer, half], dst_ref=pre_buf.at[layer, :, :, me],
            send_sem=pre_send_sem.at[layer, k], recv_sem=pre_recv_sem.at[layer, k],
            device_id={"ctx": device}, device_id_type=MESH)

    def part_send(parity, j):
        return pltpu.make_async_remote_copy(
            src_ref=own_buf.at[j], dst_ref=recv_buf.at[parity, j],
            send_sem=part_send_sem.at[j], recv_sem=part_recv_sem.at[parity, j],
            device_id={"ctx": mate}, device_id_type=MESH)

    lens_send = pltpu.make_async_remote_copy(
        src_ref=lens_ref, dst_ref=lens_buf.at[pl.ds(mine, rows)], send_sem=lens_sem.at[0], recv_sem=lens_sem.at[1],
        device_id={"ctx": mate}, device_id_type=MESH)
    kv_send = pltpu.make_async_remote_copy(
        src_ref=kv_send_buf, dst_ref=kv_out_ref.at[:, core], send_sem=kv_sem.at[0], recv_sem=kv_sem.at[1],
        device_id={"ctx": mate}, device_id_type=MESH)

    def for_tiles(body):
        lax.fori_loop(0, tiles, lambda j, _: (body(j), 0)[1], 0)

    for layer in range(2):
        for copy in suf_loads(layer):
            copy.start()

    def first_qkv(j):
        for copy in qkv_copies(0, j):
            copy.start()

    for_tiles(first_qkv)
    pre_local(0).start()
    pre_local(1).start()
    for_tiles(lambda j: wo_copy(0, j).start())

    for j in range(tiles):
        x_buf[j] = jnp.zeros_like(x_buf[j])
        own_buf[j] = jnp.zeros_like(own_buf[j])
        own_buf[j, pl.ds(mine, rows), :] = hidden_ref[:, j * TILE:(j + 1) * TILE].astype(F32)
    lens_buf[pl.ds(mine, rows)] = lens_ref[...]
    q_buf[...] = jnp.zeros_like(q_buf)
    kn_buf[...] = jnp.zeros_like(kn_buf)
    vn_buf[...] = jnp.zeros_like(vn_buf)

    barrier = pltpu.get_barrier_semaphore()
    for device, _ in peers:
        pl.semaphore_signal(barrier, inc=1, device_id={"ctx": device}, device_id_type=MESH)
    pl.semaphore_wait(barrier, 3)

    for_tiles(lambda j: part_send(1, j).start())
    lens_send.start()
    for layer in range(2):
        for k in range(3):
            pre_remote(layer, k).start()
    for copy in suf_loads(0):
        copy.wait()
    suf_send(0).start()
    lens_send.wait()

    row_ids = lax.broadcasted_iota(jnp.int32, (2 * PAD, 128), 0)
    key_ids = lax.broadcasted_iota(jnp.int32, (2 * PAD, 128), 1)
    key_slot = jnp.where(lax.rem(key_ids, 4) == 2 * core + row_ids // PAD, key_ids // 4, slots)[None]

    def update_x(parity, j):
        copy = part_send(parity, j)
        copy.wait_recv()
        copy.wait_send()
        update = (own_buf[j] + recv_buf[parity, j]).astype(BF16)
        x_buf[j] = (x_buf[j].astype(F32) + update.astype(F32)).astype(BF16)

    def layer_body(layer, carry):
        parity_in = lax.rem(layer + 1, 2)
        parity_out = lax.rem(layer, 2)

        @pl.when(layer < layers - 2)
        def _():
            for copy in suf_loads(layer + 2):
                copy.start()
            pre_local(layer + 2).start()
            for k in range(3):
                pre_remote(layer + 2, k).start()

        acc_buf[...] = jnp.zeros_like(acc_buf)

        def qkv_tile(j):
            update_x(parity_in, j)
            for copy in qkv_copies(layer, j):
                copy.wait()
            x = x_buf[j]
            acc_buf[:, 0:q_width] += jnp.dot(x, wq_buf[j], preferred_element_type=F32)
            acc_buf[:, q_width:q_width + kv_width] += jnp.dot(x, wk_buf[j], preferred_element_type=F32)
            acc_buf[:, q_width + kv_width:q_width + 2 * kv_width] += jnp.dot(x, wv_buf[j], preferred_element_type=F32)

            @pl.when(layer < layers - 1)
            def _():
                for copy in qkv_copies(layer + 1, j):
                    copy.start()

        for_tiles(qkv_tile)

        @pl.when(layer < layers - 1)
        def _():
            for copy in suf_loads(layer + 1):
                copy.wait()
            suf_send(layer + 1).start()

        for h in range(2):
            for g in range(group):
                col = (h * group + g) * head_dim
                q_buf[pl.ds(h * PAD + g, both, stride=2 * PAD), :] = acc_buf[:, col:col + head_dim].astype(BF16).astype(F32)
            k_new = acc_buf[:, q_width + h * head_dim:q_width + (h + 1) * head_dim].astype(BF16).astype(F32)
            v_col = q_width + kv_width + h * head_dim
            v_new = acc_buf[:, v_col:v_col + head_dim].astype(BF16).astype(F32)
            for g in range(PAD):
                kn_buf[pl.ds(h * PAD + g, both, stride=2 * PAD), :] = k_new
                vn_buf[pl.ds(h * PAD + g, both, stride=2 * PAD), :] = v_new
        kv_out_ref[layer, core] = acc_buf[pl.ds(mine, rows), q_width:q_width + 2 * kv_width].astype(BF16)
        kv_send_buf[layer] = acc_buf[pl.ds(other, rows), q_width:q_width + 2 * kv_width].astype(BF16)

        pre_local(layer).wait()
        for k in range(3):
            pre_remote(layer, k).wait()
        suf_send(layer).wait()

        @pl.when(layer == layers - 1)
        def _():
            kv_send.start()

        per_core = rows // CHUNK

        def attend(i, carry):
            away = i // per_core
            part = pl.multiple_of(lax.rem(i, per_core) * CHUNK, CHUNK)
            first = pl.multiple_of(lax.rem(core + away, 2) * rows + part, CHUNK)
            slot = (1 - away) * lax.rem(layer, 3) + away * (3 + lax.rem(layer, 2))
            chunk_rows = pl.ds(pl.multiple_of(first * 2 * PAD, CHUNK * 2 * PAD), CHUNK * 2 * PAD)
            q = q_buf[chunk_rows, :]
            q3 = q.reshape(CHUNK, 2 * PAD, head_dim)
            k_suf = suf_buf[slot, 0, pl.ds(part, CHUNK)]
            v_suf = suf_buf[slot, 1, pl.ds(part, CHUNK)]
            suf_scores = lax.dot_general(q3.astype(BF16), k_suf, (((2,), (2,)), ((0,), (0,))), preferred_element_type=F32) * scale
            suf_scores = jnp.where(key_slot < lens_buf[pl.ds(first, CHUNK)], suf_scores, -jnp.inf)
            k_new = kn_buf[chunk_rows, :].reshape(CHUNK, 2 * PAD, head_dim)
            v_new = vn_buf[chunk_rows, :].reshape(CHUNK, 2 * PAD, head_dim)
            new_scores = jnp.sum(q3 * k_new, axis=-1, keepdims=True) * scale
            suf_weights, new_weights, masses, pre_vals = [], [], [], []
            for h in range(2):
                hs = slice(h * PAD, (h + 1) * PAD)
                q_h = q3[:, hs, :].reshape(CHUNK * PAD, head_dim).astype(BF16)
                k_pre = pre_buf[layer, 0, h].reshape(-1, head_dim)
                v_pre = pre_buf[layer, 1, h].reshape(-1, head_dim)
                scores = lax.dot_general(q_h, k_pre, (((1,), (1,)), ((), ())), preferred_element_type=F32) * scale
                suf_h = suf_scores[:, hs, :].reshape(CHUNK * PAD, 128)
                new_h = new_scores[:, hs, :].reshape(CHUNK * PAD, 1)
                peak = jnp.maximum(jnp.maximum(scores.max(axis=-1, keepdims=True), suf_h.max(axis=-1, keepdims=True)), new_h)
                pre_w = jnp.exp(scores - peak)
                suf_w = jnp.exp(suf_h - peak)
                new_w = jnp.exp(new_h - peak)
                masses.append(pre_w.sum(axis=-1, keepdims=True) + suf_w.sum(axis=-1, keepdims=True) + new_w)
                pre_vals.append(jnp.dot(pre_w.astype(BF16), v_pre, preferred_element_type=F32))
                suf_weights.append(suf_w.reshape(CHUNK, PAD, 128))
                new_weights.append(new_w)
            suf_w = jnp.concatenate(suf_weights, axis=1).astype(BF16)
            suf_vals = lax.dot_general(suf_w, v_suf, (((2,), (1,)), ((0,), (0,))), preferred_element_type=F32)
            outs = []
            for h in range(2):
                hs = slice(h * PAD, (h + 1) * PAD)
                mixed = pre_vals[h] + suf_vals[:, hs, :].reshape(CHUNK * PAD, head_dim)
                mixed = mixed + new_weights[h] * v_new[:, hs, :].reshape(CHUNK * PAD, head_dim)
                outs.append((mixed / masses[h]).reshape(CHUNK, PAD, head_dim))
            o_buf[chunk_rows, :] = jnp.concatenate(outs, axis=1).reshape(CHUNK * 2 * PAD, head_dim)
            return carry

        lax.fori_loop(0, 2 * per_core, attend, 0)

        for h in range(2):
            for g in range(group):
                col = (h * group + g) * head_dim
                att_buf[:, col:col + head_dim] = o_buf[pl.ds(h * PAD + g, both, stride=2 * PAD), :].astype(BF16)

        def out_tile(j):
            wo_copy(layer, j).wait()
            own_buf[j] = jnp.dot(att_buf[...], wo_buf[j], preferred_element_type=F32)

            @pl.when(layer < layers - 1)
            def _():
                wo_copy(layer + 1, j).start()

            @pl.when(j > 0)
            def _():
                part_send(parity_out, j - 1).start()

        for_tiles(out_tile)
        part_send(parity_out, tiles - 1).start()
        return carry

    lax.fori_loop(0, layers, layer_body, 0)
    for j in range(tiles):
        update_x((layers - 1) % 2, j)
        out_ref[:, j * TILE:(j + 1) * TILE] = x_buf[j, pl.ds(mine, rows), :]
    kv_send.wait()


def solution(mesh):
    home_axes = ('data', 'ctx')
    row_spec = P(home_axes, None)
    lens_spec = P(home_axes)
    whole_spec = P()
    prefix_spec = P(None, home_axes, None, None)
    cache_spec = P(None, home_axes, None, None, None)

    def local_step(hidden, seq_lens, w_query, w_key, w_value, w_out, k_prefix, v_prefix, k_suffix, v_suffix):
        layers, model_dim = w_query.shape[:2]
        positions, kv_heads, head_dim = k_prefix.shape[1:]
        rows = hidden.shape[0]
        slots = k_suffix.shape[2]
        group = w_query.shape[2] // head_dim // kv_heads
        half_heads = kv_heads // 2
        q_width = w_query.shape[2] // 2
        kv_width = w_key.shape[2] // 2
        tiles = model_dim // TILE
        keys = slots * kv_heads
        both = 2 * rows

        prefix = jnp.stack([k_prefix, v_prefix]).reshape(2, layers, positions, 2, half_heads, head_dim)
        prefix = prefix.transpose(1, 3, 0, 4, 2, 5)
        lens_rep = jnp.broadcast_to(seq_lens[:, None, None], (rows, 2 * PAD, 128))
        k_flat = k_suffix.reshape(layers, rows, keys, head_dim)
        v_flat = v_suffix.reshape(layers, rows, keys, head_dim)

        any_spec = pl.BlockSpec(memory_space=pl.ANY)
        vmem_spec = pl.BlockSpec(memory_space=pltpu.VMEM)
        dma = pltpu.SemaphoreType.DMA
        hidden_out, kv_new = pl.pallas_call(
            functools.partial(decode_kernel, (layers, rows, group, head_dim, slots)),
            out_shape=(jax.ShapeDtypeStruct((rows, model_dim), BF16),
                       jax.ShapeDtypeStruct((layers, 2, rows, 2 * kv_width), BF16)),
            in_specs=[vmem_spec, vmem_spec] + [any_spec] * 7,
            out_specs=(vmem_spec, vmem_spec),
            scratch_shapes=[
                pltpu.VMEM((tiles, TILE, q_width), BF16),
                pltpu.VMEM((tiles, TILE, kv_width), BF16),
                pltpu.VMEM((tiles, TILE, kv_width), BF16),
                pltpu.VMEM((tiles, q_width, TILE), BF16),
                pltpu.VMEM((layers, 2, half_heads, 4, positions, head_dim), BF16),
                pltpu.VMEM((5, 2, rows, keys, head_dim), BF16),
                pltpu.VMEM((tiles, both, TILE), BF16),
                pltpu.VMEM((tiles, both, TILE), F32),
                pltpu.VMEM((2, tiles, both, TILE), F32),
                pltpu.VMEM((both, q_width + 2 * kv_width), F32),
                pltpu.VMEM((both * 2 * PAD, head_dim), F32),
                pltpu.VMEM((both * 2 * PAD, head_dim), F32),
                pltpu.VMEM((both * 2 * PAD, head_dim), F32),
                pltpu.VMEM((both * 2 * PAD, head_dim), F32),
                pltpu.VMEM((both, q_width), BF16),
                pltpu.VMEM((both, 2 * PAD, 128), jnp.int32),
                pltpu.VMEM((layers, rows, 2 * kv_width), BF16),
                dma((4, tiles)), dma((3, 2)), dma((2,)), dma((2,)), dma((layers,)), dma((layers, 3)), dma((layers, 3)),
                dma((tiles,)), dma((2, tiles)), dma((2,)), dma((2,)),
            ],
            compiler_params=pltpu.CompilerParams(collective_id=0, has_side_effects=True, vmem_limit_bytes=66_000_000),
            name="decode_layers",
        )(hidden, lens_rep, w_query, w_key, w_value, w_out, prefix, k_flat, v_flat)

        kv_new = kv_new.reshape(layers, 2, rows, 2, half_heads, head_dim).transpose(3, 0, 2, 1, 4, 5)
        kv_new = kv_new.reshape(2, layers, rows, 1, kv_heads, head_dim)
        hit = (lax.broadcasted_iota(jnp.int32, (rows, slots), 1) == seq_lens[:, None])[None, :, :, None, None]
        k_out = jnp.where(hit, kv_new[0], k_suffix)
        v_out = jnp.where(hit, kv_new[1], v_suffix)
        return hidden_out, k_out, v_out

    return jax.shard_map(local_step, mesh=mesh, in_specs=(row_spec, lens_spec, whole_spec, whole_spec, whole_spec, whole_spec, prefix_spec, prefix_spec, cache_spec, cache_spec), out_specs=(row_spec, cache_spec, cache_spec), check_vma=False)
```

time: 1230 us -> 231 us (0.19); the launches traced: 1210 us -> 231 us
  matrix products: 489 us -> 0 us
  blocking collectives: 201 us -> 0 us
  Pallas kernels: 0 us -> 194 us
  other arithmetic: 212 us -> 27 us
  waiting for transfers between devices: 116 us -> 0 us
  starting transfers between devices: 114 us -> 0 us
  local copies, waits for them, and re-layouts: 77.3 us -> 8.73 us
    dot_general x128 -> x0, matrix products: 489 us -> none  [the longest x16 171 us: local_step(): jnp.dot(attended, w_out[layer_idx], preferred_element_type=jnp.float32)]
    all_gather x16 -> x0, blocking collectives: 201 us -> none  [local_step(): group_queries = lax.all_gather(queries, 'ctx', axis=0, tiled=True)]
    pallas_call x0 -> x1, Pallas kernels: none -> 194 us  [local_step(): pl.pallas_call(functools.partial(decode_kernel, (layers, rows, group, hea...]
    all_to_all x32 -> x0, waiting for transfers between devices: 116 us -> none  [the longest x16 116 us: local_step(): lax.all_to_all(part_out, 'ctx', 0, 0, tiled=True)]
    all_to_all x32 -> x0, starting transfers between devices: 114 us -> none  [the longest x16 60.3 us: local_step(): lax.all_to_all(part_out, 'ctx', 0, 0, tiled=True)]
    unnamed x28 -> x0, other arithmetic: 113 us -> none
    select_n x16 -> x1, other arithmetic: 52.4 us -> 23.3 us  [local_step(): v_out = jnp.where(hit, kv_new[1], v_suffix)]
    convert_element_type x16 -> x0, local copies, waits for them, and re-layouts: 26.4 us -> none  [local_step(): part_out = (pre_vals / pre_mass[..., None]).astype(jnp.bfloat16)]
  transfers between devices with their start and end apart: 32 -> 0, of which waited for: 16 -> 0; matrix products, arithmetic and copies ran while one was open for 22% -> 0% of each run, Pallas kernels for 0% -> 0%
where the time goes in v1:
time: 231 us
  Pallas kernels  194 us (84%)
  other arithmetic  27 us (12%)
  local copies, waits for them, and re-layouts  8.73 us (4%)
    pallas_call x1, Pallas kernels, local_step(): pl.pallas_call(functools.partial(decode_kernel, (layers, rows, group, hea...  194 us
    select_n x1, other arithmetic, local_step(): v_out = jnp.where(hit, kv_new[1], v_suffix)  23.3 us
    unnamed x7, local copies, waits for them, and re-layouts  5 us

profile of v1, /device:TPU:0, one launch (start us, length us, event | category | flops | bytes accessed | tf_op | source)
XLA Modules:
  0.0 230.9 jit_solution(4084657446357274090)
XLA Ops:
  0.6 1.3 iota_compare_fusion
  2.0 1.5 broadcast_in_dim.36.lens_ref
  3.4 2.1 copy.15
  5.6 2.2 copy.16
  7.7 2.4 %maximum_bitcast_fusion.pre_ref = bf16[16,2,2,2,128,128]{5,4,3,2,1,0:T(8,128)(2,1)} fusion(bf16[1,16,128,2,2,128]{5,2,4,0,3,1:T(8,128)(2,1)S(1)} %bitcast.16, bf16[1,16,128,2,2,128]{5,2,4,0,3,1:T(8,128)(2,1)S(1)} %bitcast.15), kind=kLoop, calls=%fused_computation.2 | loop fusion | flops 2097152 | bytes 8388608 | tf_op jit(solution)/shard_map/transpose | solution.py:296
  10.1 0.0 copy-start.1
  10.1 194.4 %decode_layers.1 = (bf16[32,3584]{1,0:T(8,128)(2,1)}, bf16[16,2,32,512]{3,2,1,0:T(8,128)(2,1)}) custom-call(bf16[32,3584]{1,0:T(8,128)(2,1)} %hidden_ref.1, s32[32,16,128]{2,1,0:T(8,128)} %broadcast_in_dim.36.lens_ref, bf16[16,3584,3584]{2,1,0:T(8,128)(2,1)} %wq_ref.1, bf16[16,3584,512]{2,1,0:T(8,128)(2,1)} %wk_ref.1, bf16[16,3584,512]{2,1,0:T(8,128)(2,1)} %wv_ref.1, ...), custom_call_target="tpu_custom_call" | custom-call | tf_op jit(solution)/shard_map/decode_layers/pallas_call | solution.py:304
  204.5 1.3 reshape.48
  205.9 0.3 copy.21
  206.2 0.1 fusion
  206.3 0.3 copy.19
  206.6 0.3 copy.18
  206.8 0.0 copy-done.1
  206.8 0.0 copy-start
  206.9 23.3 %broadcast_select_fusion = (bf16[16,32,32,4,128]{4,3,2,1,0:T(4,128)(2,1)}, bf16[16,32,32,4,128]{4,3,2,1,0:T(4,128)(2,1)}) fusion(bf16[16,32,32,4,128]{4,3,2,1,0:T(4,128)(2,1)} %param.19, pred[32,32]{1,0:T(8,128)(4,1)S(1)} %copy-done.1, bf16[16,32,4,128]{3,2,1,0:T(4,128)(2,1)S(1)} %copy.19, bf16[16,32,32,4,128]{4,3,2,1,0:T(4,128)(2,1)} %param.18, ...), kind=kLoop, calls=%fused_computation | loop fusion | flops 16777216 | bytes 68158464 | tf_op jit(solution)/shard_map/jit(_where)/select_n | solution.py:339
  230.2 0.0 copy-done
  230.2 0.7 copy.23
Async XLA Ops:
  10.1 196.7 %copy-start.1 = (pred[32,32]{1,0:T(8,128)(4,1)S(1)}, pred[32,32]{1,0:T(8,128)(4,1)}, u32[]{:S(2)}) copy-start(pred[32,32]{1,0:T(8,128)(4,1)} %iota_compare_fusion) | copy-start | bytes 3076
  206.8 23.3 %copy-start = (bf16[32,3584]{1,0:T(8,128)(2,1)S(1)}, bf16[32,3584]{1,0:T(8,128)(2,1)}, u32[]{:S(2)}) copy-start(bf16[32,3584]{1,0:T(8,128)(2,1)} %get-tuple-element.14) | copy-start | bytes 688132

commit v2 on v1

--- a/solution.py
+++ b/solution.py
@@ -13,15 +13,17 @@
 TILE = 512
 CHUNK = 16
 PAD = 8
-
-
-def decode_kernel(dims, hidden_ref, lens_ref, wq_ref, wk_ref, wv_ref, wo_ref, pre_ref, ksuf_ref, vsuf_ref,
+RING = 8
+
+
+def decode_kernel(dims, lens_ref, hidden_ref, wq_ref, wk_ref, wv_ref, wo_ref, kpre_ref, vpre_ref, ksuf_ref, vsuf_ref,
                   out_ref, kv_out_ref,
-                  wq_buf, wk_buf, wv_buf, wo_buf, pre_buf, suf_buf, x_buf, own_buf, recv_buf, acc_buf, q_buf, kn_buf, vn_buf,
-                  o_buf, att_buf, lens_buf, kv_send_buf,
-                  w_sem, suf_load_sem, suf_send_sem, suf_recv_sem, pre_local_sem, pre_send_sem, pre_recv_sem,
+                  wq_buf, wk_buf, wv_buf, wo_buf, pre_buf, raw_buf, wide_buf, split_buf, suf_buf, x_buf, own_buf, recv_buf, acc_buf,
+                  q_buf, kvn_buf, o_buf, att_buf, lens_buf, kv_send_buf,
+                  w_sem, suf_load_sem, suf_send_sem, suf_recv_sem, raw_sem, pre_send_sem, pre_recv_sem,
                   part_send_sem, part_recv_sem, lens_sem, kv_sem):
     layers, rows, group, head_dim, slots = dims
+    half_heads = 2
     tiles = x_buf.shape[0]
     q_width = wq_buf.shape[2]
     kv_width = wk_buf.shape[2]
@@ -64,13 +66,30 @@
             send_sem=suf_send_sem.at[lax.rem(layer, 2)], recv_sem=suf_recv_sem.at[lax.rem(layer, 2)],
             device_id={"ctx": mate}, device_id_type=MESH)
 
-    def pre_local(layer):
-        return pltpu.make_async_copy(pre_ref.at[layer, core], pre_buf.at[layer, :, :, me], pre_local_sem.at[layer])
+    def raw_loads(layer):
+        slot = lax.rem(layer, 2)
+        return (
+            pltpu.make_async_copy(kpre_ref.at[layer], raw_buf.at[slot, 0], raw_sem.at[slot, 0]),
+            pltpu.make_async_copy(vpre_ref.at[layer], raw_buf.at[slot, 1], raw_sem.at[slot, 1]),
+        )
+
+    def split_prefix(layer):
+        slot = lax.rem(layer, 2)
+        heads = 2 * half_heads
+        positions = pre_buf.shape[4]
+        for copy in raw_loads(layer):
+            copy.wait()
+        for kv in range(2):
+            wide_buf[kv] = raw_buf[slot, kv].astype(F32)
+            for h in range(half_heads):
+                for half in range(2):
+                    split_buf[slot, half, kv, h] = wide_buf[kv, pl.ds(half * half_heads + h, positions, stride=heads), :].astype(BF16)
+                pre_buf[layer, kv, h, me] = split_buf[slot, core, kv, h]
 
     def pre_remote(layer, k):
         device, half = peers[k]
         return pltpu.make_async_remote_copy(
-            src_ref=pre_ref.at[layer, half], dst_ref=pre_buf.at[layer, :, :, me],
+            src_ref=split_buf.at[lax.rem(layer, 2), half], dst_ref=pre_buf.at[layer, :, :, me],
             send_sem=pre_send_sem.at[layer, k], recv_sem=pre_recv_sem.at[layer, k],
             device_id={"ctx": device}, device_id_type=MESH)
 
@@ -81,36 +100,45 @@
             device_id={"ctx": mate}, device_id_type=MESH)
 
     lens_send = pltpu.make_async_remote_copy(
-        src_ref=lens_ref, dst_ref=lens_buf.at[pl.ds(mine, rows)], send_sem=lens_sem.at[0], recv_sem=lens_sem.at[1],
+        src_ref=lens_buf.at[pl.ds(mine, rows)], dst_ref=lens_buf.at[pl.ds(mine, rows)], send_sem=lens_sem.at[0], recv_sem=lens_sem.at[1],
         device_id={"ctx": mate}, device_id_type=MESH)
     kv_send = pltpu.make_async_remote_copy(
-        src_ref=kv_send_buf, dst_ref=kv_out_ref.at[:, core], send_sem=kv_sem.at[0], recv_sem=kv_sem.at[1],
+        src_ref=kv_send_buf, dst_ref=kv_out_ref.at[:, :, pl.ds(core * half_heads, half_heads)], send_sem=kv_sem.at[0], recv_sem=kv_sem.at[1],
         device_id={"ctx": mate}, device_id_type=MESH)
 
     def for_tiles(body):
         lax.fori_loop(0, tiles, lambda j, _: (body(j), 0)[1], 0)
 
     for layer in range(2):
-        for copy in suf_loads(layer):
+        for copy in raw_loads(layer):
             copy.start()
+    for copy in suf_loads(0):
+        copy.start()
 
     def first_qkv(j):
         for copy in qkv_copies(0, j):
             copy.start()
 
     for_tiles(first_qkv)
-    pre_local(0).start()
-    pre_local(1).start()
     for_tiles(lambda j: wo_copy(0, j).start())
+    for copy in suf_loads(1):
+        copy.start()
 
     for j in range(tiles):
         x_buf[j] = jnp.zeros_like(x_buf[j])
         own_buf[j] = jnp.zeros_like(own_buf[j])
         own_buf[j, pl.ds(mine, rows), :] = hidden_ref[:, j * TILE:(j + 1) * TILE].astype(F32)
-    lens_buf[pl.ds(mine, rows)] = lens_ref[...]
+    diagonal_hit = lax.broadcasted_iota(jnp.int32, (rows, rows), 0) == lax.broadcasted_iota(jnp.int32, (rows, rows), 1)
+    lens_wide = jnp.broadcast_to(lens_ref[...].astype(F32), (rows, rows))
+    lens_wide = jnp.where(diagonal_hit, lens_wide, 0.0).sum(axis=1, keepdims=True)
+    lens_wide = jnp.broadcast_to(lens_wide, (rows, 128)).astype(jnp.int32)
+    for b in range(rows):
+        lens_buf[mine + b] = jnp.broadcast_to(lens_wide[b:b + 1, :], (2 * PAD, 128))
     q_buf[...] = jnp.zeros_like(q_buf)
-    kn_buf[...] = jnp.zeros_like(kn_buf)
-    vn_buf[...] = jnp.zeros_like(vn_buf)
+    split_prefix(0)
+    for copy in raw_loads(2):
+        copy.start()
+    split_prefix(1)
 
     barrier = pltpu.get_barrier_semaphore()
     for device, _ in peers:
@@ -142,13 +170,19 @@
         parity_in = lax.rem(layer + 1, 2)
         parity_out = lax.rem(layer, 2)
 
+        @pl.when(layer < layers - 3)
+        def _():
+            for copy in raw_loads(layer + 3):
+                copy.start()
+
+        for k in range(3):
+            pre_remote(layer, k).wait_send()
+
         @pl.when(layer < layers - 2)
         def _():
             for copy in suf_loads(layer + 2):
                 copy.start()
-            pre_local(layer + 2).start()
-            for k in range(3):
-                pre_remote(layer + 2, k).start()
+            split_prefix(layer + 2)
 
         acc_buf[...] = jnp.zeros_like(acc_buf)
 
@@ -166,30 +200,36 @@
                 for copy in qkv_copies(layer + 1, j):
                     copy.start()
 
+            @pl.when(j == 1)
+            def _():
+                @pl.when(layer < layers - 1)
+                def _():
+                    for copy in suf_loads(layer + 1):
+                        copy.wait()
+                    suf_send(layer + 1).start()
+
+                @pl.when(layer < layers - 2)
+                def _():
+                    for k in range(3):
+                        pre_remote(layer + 2, k).start()
+
         for_tiles(qkv_tile)
-
-        @pl.when(layer < layers - 1)
-        def _():
-            for copy in suf_loads(layer + 1):
-                copy.wait()
-            suf_send(layer + 1).start()
 
         for h in range(2):
             for g in range(group):
                 col = (h * group + g) * head_dim
                 q_buf[pl.ds(h * PAD + g, both, stride=2 * PAD), :] = acc_buf[:, col:col + head_dim].astype(BF16).astype(F32)
-            k_new = acc_buf[:, q_width + h * head_dim:q_width + (h + 1) * head_dim].astype(BF16).astype(F32)
-            v_col = q_width + kv_width + h * head_dim
-            v_new = acc_buf[:, v_col:v_col + head_dim].astype(BF16).astype(F32)
-            for g in range(PAD):
-                kn_buf[pl.ds(h * PAD + g, both, stride=2 * PAD), :] = k_new
-                vn_buf[pl.ds(h * PAD + g, both, stride=2 * PAD), :] = v_new
-        kv_out_ref[layer, core] = acc_buf[pl.ds(mine, rows), q_width:q_width + 2 * kv_width].astype(BF16)
-        kv_send_buf[layer] = acc_buf[pl.ds(other, rows), q_width:q_width + 2 * kv_width].astype(BF16)
-
-        pre_local(layer).wait()
+            for kv in range(2):
+                col = q_width + kv * kv_width + h * head_dim
+                fresh = acc_buf[:, col:col + head_dim].astype(BF16).astype(F32)
+                kvn_buf[kv, h] = fresh
+        for h in range(2):
+            for kv in range(2):
+                kv_out_ref[layer, kv, core * half_heads + h] = kvn_buf[kv, h, pl.ds(mine, rows), :]
+                kv_send_buf[layer, kv, h] = kvn_buf[kv, h, pl.ds(other, rows), :]
+
         for k in range(3):
-            pre_remote(layer, k).wait()
+            pre_remote(layer, k).wait_recv()
         suf_send(layer).wait()
 
         @pl.when(layer == layers - 1)
@@ -210,8 +250,12 @@
             v_suf = suf_buf[slot, 1, pl.ds(part, CHUNK)]
             suf_scores = lax.dot_general(q3.astype(BF16), k_suf, (((2,), (2,)), ((0,), (0,))), preferred_element_type=F32) * scale
             suf_scores = jnp.where(key_slot < lens_buf[pl.ds(first, CHUNK)], suf_scores, -jnp.inf)
-            k_new = kn_buf[chunk_rows, :].reshape(CHUNK, 2 * PAD, head_dim)
-            v_new = vn_buf[chunk_rows, :].reshape(CHUNK, 2 * PAD, head_dim)
+            def spread(kv):
+                picked = [jnp.broadcast_to(kvn_buf[kv, h, pl.ds(first + b, 1), :], (PAD, head_dim)) for b in range(CHUNK) for h in range(2)]
+                return jnp.concatenate(picked, axis=0).reshape(CHUNK, 2 * PAD, head_dim)
+
+            k_new = spread(0)
+            v_new = spread(1)
             new_scores = jnp.sum(q3 * k_new, axis=-1, keepdims=True) * scale
             suf_weights, new_weights, masses, pre_vals = [], [], [], []
             for h in range(2):
@@ -271,6 +315,57 @@
     kv_send.wait()
 
 
+def cache_kernel(lens_ref, new_ref, k_ref, v_ref, k_out_ref, v_out_ref, buf, new_buf, in_sem, out_sem, new_sem):
+    layers, rows, _, heads, _ = k_ref.shape
+    ahead = RING // 2
+
+    def loads(layer):
+        slot = lax.rem(layer, RING)
+        return (
+            pltpu.make_async_copy(k_ref.at[layer], buf.at[slot, 0], in_sem.at[slot, 0]),
+            pltpu.make_async_copy(v_ref.at[layer], buf.at[slot, 1], in_sem.at[slot, 1]),
+            pltpu.make_async_copy(new_ref.at[layer], new_buf.at[slot], new_sem.at[slot]),
+        )
+
+    def stores(layer):
+        slot = lax.rem(layer, RING)
+        return (
+            pltpu.make_async_copy(buf.at[slot, 0], k_out_ref.at[layer], out_sem.at[slot, 0]),
+            pltpu.make_async_copy(buf.at[slot, 1], v_out_ref.at[layer], out_sem.at[slot, 1]),
+        )
+
+    for layer in range(ahead):
+        for copy in loads(layer):
+            copy.start()
+
+    def step(layer, carry):
+        slot = lax.rem(layer, RING)
+
+        @pl.when(layer >= ahead)
+        def _():
+            for copy in stores(layer - ahead):
+                copy.wait()
+
+        @pl.when(layer < layers - ahead)
+        def _():
+            for copy in loads(layer + ahead):
+                copy.start()
+
+        for copy in loads(layer):
+            copy.wait()
+        for b in range(rows):
+            for kv in range(2):
+                buf[slot, kv, b, lens_ref[b]] = new_buf[slot, kv, pl.ds(b, heads, stride=rows), :].astype(BF16)
+        for copy in stores(layer):
+            copy.start()
+        return carry
+
+    lax.fori_loop(0, layers, step, 0)
+    for layer in range(layers - ahead, layers):
+        for copy in stores(layer):
+            copy.wait()
+
+
 def solution(mesh):
     home_axes = ('data', 'ctx')
     row_spec = P(home_axes, None)
@@ -292,20 +387,20 @@
         keys = slots * kv_heads
         both = 2 * rows
 
-        prefix = jnp.stack([k_prefix, v_prefix]).reshape(2, layers, positions, 2, half_heads, head_dim)
-        prefix = prefix.transpose(1, 3, 0, 4, 2, 5)
-        lens_rep = jnp.broadcast_to(seq_lens[:, None, None], (rows, 2 * PAD, 128))
         k_flat = k_suffix.reshape(layers, rows, keys, head_dim)
         v_flat = v_suffix.reshape(layers, rows, keys, head_dim)
+        k_pre = k_prefix.reshape(layers, positions * kv_heads, head_dim)
+        v_pre = v_prefix.reshape(layers, positions * kv_heads, head_dim)
 
         any_spec = pl.BlockSpec(memory_space=pl.ANY)
+        smem_spec = pl.BlockSpec(memory_space=pltpu.SMEM)
         vmem_spec = pl.BlockSpec(memory_space=pltpu.VMEM)
         dma = pltpu.SemaphoreType.DMA
         hidden_out, kv_new = pl.pallas_call(
             functools.partial(decode_kernel, (layers, rows, group, head_dim, slots)),
             out_shape=(jax.ShapeDtypeStruct((rows, model_dim), BF16),
-                       jax.ShapeDtypeStruct((layers, 2, rows, 2 * kv_width), BF16)),
-            in_specs=[vmem_spec, vmem_spec] + [any_spec] * 7,
+                       jax.ShapeDtypeStruct((layers, 2, kv_heads, rows, head_dim), F32)),
+            in_specs=[vmem_spec, vmem_spec] + [any_spec] * 8,
             out_specs=(vmem_spec, vmem_spec),
             scratch_shapes=[
                 pltpu.VMEM((tiles, TILE, q_width), BF16),
@@ -313,30 +408,40 @@
                 pltpu.VMEM((tiles, TILE, kv_width), BF16),
                 pltpu.VMEM((tiles, q_width, TILE), BF16),
                 pltpu.VMEM((layers, 2, half_heads, 4, positions, head_dim), BF16),
+                pltpu.VMEM((2, 2, positions * kv_heads, head_dim), BF16),
+                pltpu.VMEM((2, positions * kv_heads, head_dim), F32),
+                pltpu.VMEM((2, 2, 2, half_heads, positions, head_dim), BF16),
                 pltpu.VMEM((5, 2, rows, keys, head_dim), BF16),
                 pltpu.VMEM((tiles, both, TILE), BF16),
                 pltpu.VMEM((tiles, both, TILE), F32),
                 pltpu.VMEM((2, tiles, both, TILE), F32),
                 pltpu.VMEM((both, q_width + 2 * kv_width), F32),
                 pltpu.VMEM((both * 2 * PAD, head_dim), F32),
-                pltpu.VMEM((both * 2 * PAD, head_dim), F32),
-                pltpu.VMEM((both * 2 * PAD, head_dim), F32),
+                pltpu.VMEM((2, half_heads, both, head_dim), F32),
                 pltpu.VMEM((both * 2 * PAD, head_dim), F32),
                 pltpu.VMEM((both, q_width), BF16),
                 pltpu.VMEM((both, 2 * PAD, 128), jnp.int32),
-                pltpu.VMEM((layers, rows, 2 * kv_width), BF16),
-                dma((4, tiles)), dma((3, 2)), dma((2,)), dma((2,)), dma((layers,)), dma((layers, 3)), dma((layers, 3)),
+                pltpu.VMEM((layers, 2, half_heads, rows, head_dim), F32),
+                dma((4, tiles)), dma((3, 2)), dma((2,)), dma((2,)), dma((2, 2)), dma((layers, 3)), dma((layers, 3)),
                 dma((tiles,)), dma((2, tiles)), dma((2,)), dma((2,)),
             ],
             compiler_params=pltpu.CompilerParams(collective_id=0, has_side_effects=True, vmem_limit_bytes=66_000_000),
             name="decode_layers",
-        )(hidden, lens_rep, w_query, w_key, w_value, w_out, prefix, k_flat, v_flat)
-
-        kv_new = kv_new.reshape(layers, 2, rows, 2, half_heads, head_dim).transpose(3, 0, 2, 1, 4, 5)
-        kv_new = kv_new.reshape(2, layers, rows, 1, kv_heads, head_dim)
-        hit = (lax.broadcasted_iota(jnp.int32, (rows, slots), 1) == seq_lens[:, None])[None, :, :, None, None]
-        k_out = jnp.where(hit, kv_new[0], k_suffix)
-        v_out = jnp.where(hit, kv_new[1], v_suffix)
+        )(seq_lens.reshape(1, rows), hidden, w_query, w_key, w_value, w_out, k_pre, v_pre, k_flat, v_flat)
+
+        k_out, v_out = pl.pallas_call(
+            cache_kernel,
+            out_shape=(jax.ShapeDtypeStruct(k_suffix.shape, BF16), jax.ShapeDtypeStruct(v_suffix.shape, BF16)),
+            in_specs=[smem_spec] + [any_spec] * 3,
+            out_specs=(any_spec, any_spec),
+            scratch_shapes=[
+                pltpu.VMEM((RING, 2) + k_suffix.shape[1:], BF16),
+                pltpu.VMEM((RING, 2, kv_heads * rows, head_dim), F32),
+                dma((RING, 2)), dma((RING, 2)), dma((RING,)),
+            ],
+            compiler_params=pltpu.CompilerParams(vmem_limit_bytes=60_000_000),
+            name="write_caches",
+        )(seq_lens, kv_new.reshape(layers, 2, kv_heads * rows, head_dim), k_suffix, v_suffix)
         return hidden_out, k_out, v_out
 
     return jax.shard_map(local_step, mesh=mesh, in_specs=(row_spec, lens_spec, whole_spec, whole_spec, whole_spec, whole_spec, prefix_spec, prefix_spec, cache_spec, cache_spec), out_specs=(row_spec, cache_spec, cache_spec), check_vma=False)

time: 231 us -> 223 us (0.965)
  Pallas kernels: 194 us -> 222 us
  other arithmetic: 27 us -> 0 us
  local copies, waits for them, and re-layouts: 8.73 us -> 0.69 us
    pallas_call x0 -> x1, Pallas kernels: none -> 23.9 us  [local_step(): pl.pallas_call(cache_kernel, out_shape=(jax.ShapeDtypeStruct(k_suffix.sha...]
    select_n x1 -> x0, other arithmetic: 23.3 us -> none  [local_step(): v_out = jnp.where(hit, kv_new[1], v_suffix)]
    unnamed x7 -> x3, local copies, waits for them, and re-layouts: 5 us -> 0.69 us
    pallas_call x1, Pallas kernels: 194 us -> 198 us  [local_step(): pl.pallas_call(functools.partial(decode_kernel, (layers, rows, group, hea...]
    transpose x1 -> x0, other arithmetic: 2.38 us -> none  [local_step(): prefix = prefix.transpose(1, 3, 0, 4, 2, 5)]
where the time goes in v2:
time: 223 us
  Pallas kernels  222 us (100%)
    pallas_call x1, Pallas kernels, local_step(): pl.pallas_call(functools.partial(decode_kernel, (layers, rows, group, hea...  198 us
    pallas_call x1, Pallas kernels, local_step(): pl.pallas_call(cache_kernel, out_shape=(jax.ShapeDtypeStruct(k_suffix.sha...  23.9 us

profile of v2, /device:TPU:0, one launch (start us, length us, event | category | flops | bytes accessed | tf_op | source)
XLA Modules:
  0.0 222.9 jit_solution(10279214257240559172)
XLA Ops:
  0.6 197.6 %decode_layers.1 = (bf16[32,3584]{1,0:T(8,128)(2,1)}, f32[16,2,4,32,128]{4,3,2,1,0:T(8,128)}) custom-call(s32[1,32]{1,0:T(1,128)} %bitcast.11, bf16[32,3584]{1,0:T(8,128)(2,1)} %hidden_ref.1, bf16[16,3584,3584]{2,1,0:T(8,128)(2,1)} %wq_ref.1, bf16[16,3584,512]{2,1,0:T(8,128)(2,1)} %wk_ref.1, bf16[16,3584,512]{2,1,0:T(8,128)(2,1)} %wv_ref.1, ...), custom_call_target="tpu_custom_call" | custom-call | tf_op jit(solution)/shard_map/decode_layers/pallas_call | solution.py:399
  198.3 0.0 copy-start
  198.3 23.9 %write_caches.1 = (bf16[16,32,32,4,128]{4,3,2,1,0:T(4,128)(2,1)}, bf16[16,32,32,4,128]{4,3,2,1,0:T(4,128)(2,1)}) custom-call(s32[32]{0:T(128)} %lens_ref.1, f32[16,2,128,128]{3,2,1,0:T(8,128)} %bitcast.10, bf16[16,32,32,4,128]{4,3,2,1,0:T(4,128)(2,1)} %k_ref.1, bf16[16,32,32,4,128]{4,3,2,1,0:T(4,128)(2,1)} %v_ref.1), custom_call_target="tpu_custom_call" | custom-call | tf_op jit(solution)/shard_map/write_caches/pallas_call | solution.py:432
  222.2 0.0 copy-done
  222.2 0.7 copy.14
Async XLA Ops:
  198.3 23.9 %copy-start = (bf16[32,3584]{1,0:T(8,128)(2,1)S(1)}, bf16[32,3584]{1,0:T(8,128)(2,1)}, u32[]{:S(2)}) copy-start(bf16[32,3584]{1,0:T(8,128)(2,1)} %get-tuple-element.14) | copy-start | bytes 688132

commit v3 on v2

--- a/solution.py
+++ b/solution.py
@@ -14,6 +14,8 @@
 CHUNK = 16
 PAD = 8
 RING = 8
+BLOCK = 2
+CHUNKS_PER_TRIP = 2
 
 
 def decode_kernel(dims, lens_ref, hidden_ref, wq_ref, wk_ref, wv_ref, wo_ref, kpre_ref, vpre_ref, ksuf_ref, vsuf_ref,
@@ -24,9 +26,10 @@
                   part_send_sem, part_recv_sem, lens_sem, kv_sem):
     layers, rows, group, head_dim, slots = dims
     half_heads = 2
-    tiles = x_buf.shape[0]
-    q_width = wq_buf.shape[2]
-    kv_width = wk_buf.shape[2]
+    tiles = own_buf.shape[0]
+    q_width = wq_buf.shape[1]
+    kv_width = wk_buf.shape[1]
+    blocks = [(a, min(a + BLOCK, tiles)) for a in range(0, tiles, BLOCK)]
     both = 2 * rows
     me = lax.axis_index("ctx")
     core = lax.rem(me, 2)
@@ -41,17 +44,19 @@
     kv_col = pl.multiple_of(core * kv_width, 128)
     scale = head_dim ** -0.5
 
-    def qkv_copies(layer, j):
-        r = pl.ds(pl.multiple_of(j * TILE, TILE), TILE)
+    def qkv_copies(layer, i):
+        a, b = blocks[i]
+        r = pl.ds(a * TILE, (b - a) * TILE)
         return (
-            pltpu.make_async_copy(wq_ref.at[layer, r, pl.ds(q_col, q_width)], wq_buf.at[j], w_sem.at[0, j]),
-            pltpu.make_async_copy(wk_ref.at[layer, r, pl.ds(kv_col, kv_width)], wk_buf.at[j], w_sem.at[1, j]),
-            pltpu.make_async_copy(wv_ref.at[layer, r, pl.ds(kv_col, kv_width)], wv_buf.at[j], w_sem.at[2, j]),
+            pltpu.make_async_copy(wq_ref.at[layer, r, pl.ds(q_col, q_width)], wq_buf.at[r], w_sem.at[0, i]),
+            pltpu.make_async_copy(wk_ref.at[layer, r, pl.ds(kv_col, kv_width)], wk_buf.at[r], w_sem.at[1, i]),
+            pltpu.make_async_copy(wv_ref.at[layer, r, pl.ds(kv_col, kv_width)], wv_buf.at[r], w_sem.at[2, i]),
         )
 
-    def wo_copy(layer, j):
-        cols = pl.ds(pl.multiple_of(j * TILE, TILE), TILE)
-        return pltpu.make_async_copy(wo_ref.at[layer, pl.ds(q_col, q_width), cols], wo_buf.at[j], w_sem.at[3, j])
+    def wo_copy(layer, i):
+        a, b = blocks[i]
+        cols = pl.ds(a * TILE, (b - a) * TILE)
+        return pltpu.make_async_copy(wo_ref.at[layer, pl.ds(q_col, q_width), cols], wo_buf.at[:, cols], w_sem.at[3, i])
 
     def suf_loads(layer):
         slot = lax.rem(layer, 3)
@@ -106,26 +111,22 @@
         src_ref=kv_send_buf, dst_ref=kv_out_ref.at[:, :, pl.ds(core * half_heads, half_heads)], send_sem=kv_sem.at[0], recv_sem=kv_sem.at[1],
         device_id={"ctx": mate}, device_id_type=MESH)
 
-    def for_tiles(body):
-        lax.fori_loop(0, tiles, lambda j, _: (body(j), 0)[1], 0)
-
     for layer in range(2):
         for copy in raw_loads(layer):
             copy.start()
     for copy in suf_loads(0):
         copy.start()
 
-    def first_qkv(j):
-        for copy in qkv_copies(0, j):
+    for i in range(len(blocks)):
+        for copy in qkv_copies(0, i):
             copy.start()
-
-    for_tiles(first_qkv)
-    for_tiles(lambda j: wo_copy(0, j).start())
+    for i in range(len(blocks)):
+        wo_copy(0, i).start()
     for copy in suf_loads(1):
         copy.start()
 
+    x_buf[...] = jnp.zeros_like(x_buf)
     for j in range(tiles):
-        x_buf[j] = jnp.zeros_like(x_buf[j])
         own_buf[j] = jnp.zeros_like(own_buf[j])
         own_buf[j, pl.ds(mine, rows), :] = hidden_ref[:, j * TILE:(j + 1) * TILE].astype(F32)
     diagonal_hit = lax.broadcasted_iota(jnp.int32, (rows, rows), 0) == lax.broadcasted_iota(jnp.int32, (rows, rows), 1)
@@ -145,7 +146,8 @@
         pl.semaphore_signal(barrier, inc=1, device_id={"ctx": device}, device_id_type=MESH)
     pl.semaphore_wait(barrier, 3)
 
-    for_tiles(lambda j: part_send(1, j).start())
+    for j in range(tiles):
+        part_send(1, j).start()
     lens_send.start()
     for layer in range(2):
         for k in range(3):
@@ -164,7 +166,8 @@
         copy.wait_recv()
         copy.wait_send()
         update = (own_buf[j] + recv_buf[parity, j]).astype(BF16)
-        x_buf[j] = (x_buf[j].astype(F32) + update.astype(F32)).astype(BF16)
+        cols = slice(j * TILE, (j + 1) * TILE)
+        x_buf[:, cols] = (x_buf[:, cols].astype(F32) + update.astype(F32)).astype(BF16)
 
     def layer_body(layer, carry):
         parity_in = lax.rem(layer + 1, 2)
@@ -184,36 +187,37 @@
                 copy.start()
             split_prefix(layer + 2)
 
-        acc_buf[...] = jnp.zeros_like(acc_buf)
-
-        def qkv_tile(j):
-            update_x(parity_in, j)
-            for copy in qkv_copies(layer, j):
-                copy.wait()
-            x = x_buf[j]
-            acc_buf[:, 0:q_width] += jnp.dot(x, wq_buf[j], preferred_element_type=F32)
-            acc_buf[:, q_width:q_width + kv_width] += jnp.dot(x, wk_buf[j], preferred_element_type=F32)
-            acc_buf[:, q_width + kv_width:q_width + 2 * kv_width] += jnp.dot(x, wv_buf[j], preferred_element_type=F32)
+        for i, (a, b) in enumerate(blocks):
+            if i == 0:
+                for copy in qkv_copies(layer, 0):
+                    copy.wait()
+            if i + 1 < len(blocks):
+                for copy in qkv_copies(layer, i + 1):
+                    copy.wait()
+            for j in range(a, b):
+                update_x(parity_in, j)
+            r = slice(a * TILE, b * TILE)
+            x = x_buf[:, r]
+            parts = ((slice(0, q_width), wq_buf), (slice(q_width, q_width + kv_width), wk_buf),
+                     (slice(q_width + kv_width, q_width + 2 * kv_width), wv_buf))
+            for cols, w_buf in parts:
+                product = jnp.dot(x, w_buf[r, :], preferred_element_type=F32)
+                acc_buf[:, cols] = product if i == 0 else acc_buf[:, cols] + product
 
             @pl.when(layer < layers - 1)
             def _():
-                for copy in qkv_copies(layer + 1, j):
+                for copy in qkv_copies(layer + 1, i):
                     copy.start()
-
-            @pl.when(j == 1)
-            def _():
-                @pl.when(layer < layers - 1)
-                def _():
+                if i == 0:
                     for copy in suf_loads(layer + 1):
                         copy.wait()
                     suf_send(layer + 1).start()
 
+            if i == 0:
                 @pl.when(layer < layers - 2)
                 def _():
                     for k in range(3):
                         pre_remote(layer + 2, k).start()
-
-        for_tiles(qkv_tile)
 
         for h in range(2):
             for g in range(group):
@@ -238,7 +242,12 @@
 
         per_core = rows // CHUNK
 
-        def attend(i, carry):
+        def unpair(both_seqs):
+            first_seq = both_seqs[:, None, 0:2 * PAD, 0:128]
+            second_seq = both_seqs[:, None, 2 * PAD:4 * PAD, 128:256]
+            return jnp.concatenate([first_seq, second_seq], axis=1).reshape(CHUNK, 2 * PAD, 128)
+
+        def attend(i):
             away = i // per_core
             part = pl.multiple_of(lax.rem(i, per_core) * CHUNK, CHUNK)
             first = pl.multiple_of(lax.rem(core + away, 2) * rows + part, CHUNK)
@@ -248,7 +257,9 @@
             q3 = q.reshape(CHUNK, 2 * PAD, head_dim)
             k_suf = suf_buf[slot, 0, pl.ds(part, CHUNK)]
             v_suf = suf_buf[slot, 1, pl.ds(part, CHUNK)]
-            suf_scores = lax.dot_general(q3.astype(BF16), k_suf, (((2,), (2,)), ((0,), (0,))), preferred_element_type=F32) * scale
+            q_pairs = q3.astype(BF16).reshape(CHUNK // 2, 4 * PAD, head_dim)
+            k_pairs = k_suf.reshape(CHUNK // 2, 256, head_dim)
+            suf_scores = unpair(lax.dot_general(q_pairs, k_pairs, (((2,), (2,)), ((0,), (0,))), preferred_element_type=F32)) * scale
             suf_scores = jnp.where(key_slot < lens_buf[pl.ds(first, CHUNK)], suf_scores, -jnp.inf)
             def spread(kv):
                 picked = [jnp.broadcast_to(kvn_buf[kv, h, pl.ds(first + b, 1), :], (PAD, head_dim)) for b in range(CHUNK) for h in range(2)]
@@ -275,7 +286,10 @@
                 suf_weights.append(suf_w.reshape(CHUNK, PAD, 128))
                 new_weights.append(new_w)
             suf_w = jnp.concatenate(suf_weights, axis=1).astype(BF16)
-            suf_vals = lax.dot_general(suf_w, v_suf, (((2,), (1,)), ((0,), (0,))), preferred_element_type=F32)
+            v_suf = v_suf.reshape(CHUNK // 2, 2, 128, head_dim)
+            v_pairs = jnp.concatenate([v_suf[:, 0], v_suf[:, 1]], axis=-1)
+            suf_w = suf_w.reshape(CHUNK // 2, 4 * PAD, 128)
+            suf_vals = unpair(lax.dot_general(suf_w, v_pairs, (((2,), (1,)), ((0,), (0,))), preferred_element_type=F32))
             outs = []
             for h in range(2):
                 hs = slice(h * PAD, (h + 1) * PAD)
@@ -283,35 +297,40 @@
                 mixed = mixed + new_weights[h] * v_new[:, hs, :].reshape(CHUNK * PAD, head_dim)
                 outs.append((mixed / masses[h]).reshape(CHUNK, PAD, head_dim))
             o_buf[chunk_rows, :] = jnp.concatenate(outs, axis=1).reshape(CHUNK * 2 * PAD, head_dim)
+
+        def attend_trip(trip, carry):
+            for i in range(CHUNKS_PER_TRIP):
+                attend(trip * CHUNKS_PER_TRIP + i)
             return carry
 
-        lax.fori_loop(0, 2 * per_core, attend, 0)
+        lax.fori_loop(0, 2 * per_core // CHUNKS_PER_TRIP, attend_trip, 0)
+        wo_copy(layer, 0).wait()
 
         for h in range(2):
             for g in range(group):
                 col = (h * group + g) * head_dim
                 att_buf[:, col:col + head_dim] = o_buf[pl.ds(h * PAD + g, both, stride=2 * PAD), :].astype(BF16)
 
-        def out_tile(j):
-            wo_copy(layer, j).wait()
-            own_buf[j] = jnp.dot(att_buf[...], wo_buf[j], preferred_element_type=F32)
+        for i, (a, b) in enumerate(blocks):
+            if i + 1 < len(blocks):
+                wo_copy(layer, i + 1).wait()
+            product = jnp.dot(att_buf[...], wo_buf[:, a * TILE:b * TILE], preferred_element_type=F32)
+            for j in range(a, b):
+                own_buf[j] = product[:, (j - a) * TILE:(j - a + 1) * TILE]
 
             @pl.when(layer < layers - 1)
             def _():
-                wo_copy(layer + 1, j).start()
-
-            @pl.when(j > 0)
-            def _():
-                part_send(parity_out, j - 1).start()
-
-        for_tiles(out_tile)
-        part_send(parity_out, tiles - 1).start()
+                wo_copy(layer + 1, i).start()
+
+            for j in range(a, b):
+                part_send(parity_out, j).start()
+
         return carry
 
     lax.fori_loop(0, layers, layer_body, 0)
     for j in range(tiles):
         update_x((layers - 1) % 2, j)
-        out_ref[:, j * TILE:(j + 1) * TILE] = x_buf[j, pl.ds(mine, rows), :]
+        out_ref[:, j * TILE:(j + 1) * TILE] = x_buf[pl.ds(mine, rows), j * TILE:(j + 1) * TILE]
     kv_send.wait()
 
 
@@ -403,16 +422,16 @@
             in_specs=[vmem_spec, vmem_spec] + [any_spec] * 8,
             out_specs=(vmem_spec, vmem_spec),
             scratch_shapes=[
-                pltpu.VMEM((tiles, TILE, q_width), BF16),
-                pltpu.VMEM((tiles, TILE, kv_width), BF16),
-                pltpu.VMEM((tiles, TILE, kv_width), BF16),
-                pltpu.VMEM((tiles, q_width, TILE), BF16),
+                pltpu.VMEM((model_dim, q_width), BF16),
+                pltpu.VMEM((model_dim, kv_width), BF16),
+                pltpu.VMEM((model_dim, kv_width), BF16),
+                pltpu.VMEM((q_width, model_dim), BF16),
                 pltpu.VMEM((layers, 2, half_heads, 4, positions, head_dim), BF16),
                 pltpu.VMEM((2, 2, positions * kv_heads, head_dim), BF16),
                 pltpu.VMEM((2, positions * kv_heads, head_dim), F32),
                 pltpu.VMEM((2, 2, 2, half_heads, positions, head_dim), BF16),
                 pltpu.VMEM((5, 2, rows, keys, head_dim), BF16),
-                pltpu.VMEM((tiles, both, TILE), BF16),
+                pltpu.VMEM((both, model_dim), BF16),
                 pltpu.VMEM((tiles, both, TILE), F32),
                 pltpu.VMEM((2, tiles, both, TILE), F32),
                 pltpu.VMEM((both, q_width + 2 * kv_width), F32),
@@ -422,7 +441,7 @@
                 pltpu.VMEM((both, q_width), BF16),
                 pltpu.VMEM((both, 2 * PAD, 128), jnp.int32),
                 pltpu.VMEM((layers, 2, half_heads, rows, head_dim), F32),
-                dma((4, tiles)), dma((3, 2)), dma((2,)), dma((2,)), dma((2, 2)), dma((layers, 3)), dma((layers, 3)),
+                dma((4, -(-tiles // BLOCK))), dma((3, 2)), dma((2,)), dma((2,)), dma((2, 2)), dma((layers, 3)), dma((layers, 3)),
                 dma((tiles,)), dma((2, tiles)), dma((2,)), dma((2,)),
             ],
             compiler_params=pltpu.CompilerParams(collective_id=0, has_side_effects=True, vmem_limit_bytes=66_000_000),

time: 223 us -> 194 us (0.87)
  Pallas kernels: 222 us -> 192 us
    pallas_call x1, Pallas kernels: 198 us -> 168 us  [local_step(): pl.pallas_call(functools.partial(decode_kernel, (layers, rows, group, hea...]
where the time goes in v3:
time: 194 us
  Pallas kernels  192 us (99%)
    pallas_call x1, Pallas kernels, local_step(): pl.pallas_call(functools.partial(decode_kernel, (layers, rows, group, hea...  168 us
    pallas_call x1, Pallas kernels, local_step(): pl.pallas_call(cache_kernel, out_shape=(jax.ShapeDtypeStruct(k_suffix.sha...  23.9 us

profile of v3, /device:TPU:0, one launch (start us, length us, event | category | flops | bytes accessed | tf_op | source)
XLA Modules:
  0.0 193.6 jit_solution(17612620757927859431)
XLA Ops:
  0.6 168.3 %decode_layers.1 = (bf16[32,3584]{1,0:T(8,128)(2,1)}, f32[16,2,4,32,128]{4,3,2,1,0:T(8,128)}) custom-call(s32[1,32]{1,0:T(1,128)} %bitcast.11, bf16[32,3584]{1,0:T(8,128)(2,1)} %hidden_ref.1, bf16[16,3584,3584]{2,1,0:T(8,128)(2,1)} %wq_ref.1, bf16[16,3584,512]{2,1,0:T(8,128)(2,1)} %wk_ref.1, bf16[16,3584,512]{2,1,0:T(8,128)(2,1)} %wv_ref.1, ...), custom_call_target="tpu_custom_call" | custom-call | tf_op jit(solution)/shard_map/decode_layers/pallas_call | solution.py:418
  169.0 0.0 copy-start
  169.0 23.9 %write_caches.1 = (bf16[16,32,32,4,128]{4,3,2,1,0:T(4,128)(2,1)}, bf16[16,32,32,4,128]{4,3,2,1,0:T(4,128)(2,1)}) custom-call(s32[32]{0:T(128)} %lens_ref.1, f32[16,2,128,128]{3,2,1,0:T(8,128)} %bitcast.10, bf16[16,32,32,4,128]{4,3,2,1,0:T(4,128)(2,1)} %k_ref.1, bf16[16,32,32,4,128]{4,3,2,1,0:T(4,128)(2,1)} %v_ref.1), custom_call_target="tpu_custom_call" | custom-call | tf_op jit(solution)/shard_map/write_caches/pallas_call | solution.py:451
  192.9 0.0 copy-done
  192.9 0.7 copy.14
Async XLA Ops:
  169.0 23.9 %copy-start = (bf16[32,3584]{1,0:T(8,128)(2,1)S(1)}, bf16[32,3584]{1,0:T(8,128)(2,1)}, u32[]{:S(2)}) copy-start(bf16[32,3584]{1,0:T(8,128)(2,1)} %get-tuple-element.14) | copy-start | bytes 688132

commit v4 on v3

--- a/solution.py
+++ b/solution.py
@@ -11,17 +11,18 @@
 BF16 = jnp.bfloat16
 F32 = jnp.float32
 TILE = 512
-CHUNK = 16
+CHUNK = 32
 PAD = 8
 RING = 8
 BLOCK = 2
-CHUNKS_PER_TRIP = 2
+LOG2E = 1.4426950408889634
+CHUNKS_PER_TRIP = 1
 
 
 def decode_kernel(dims, lens_ref, hidden_ref, wq_ref, wk_ref, wv_ref, wo_ref, kpre_ref, vpre_ref, ksuf_ref, vsuf_ref,
                   out_ref, kv_out_ref,
                   wq_buf, wk_buf, wv_buf, wo_buf, pre_buf, raw_buf, wide_buf, split_buf, suf_buf, x_buf, own_buf, recv_buf, acc_buf,
-                  q_buf, kvn_buf, o_buf, att_buf, lens_buf, kv_send_buf,
+                  q_buf, kvn_buf, o_buf, att_buf, lens_buf, kv_mine_buf, kv_send_buf,
                   w_sem, suf_load_sem, suf_send_sem, suf_recv_sem, raw_sem, pre_send_sem, pre_recv_sem,
                   part_send_sem, part_recv_sem, lens_sem, kv_sem):
     layers, rows, group, head_dim, slots = dims
@@ -107,19 +108,21 @@
     lens_send = pltpu.make_async_remote_copy(
         src_ref=lens_buf.at[pl.ds(mine, rows)], dst_ref=lens_buf.at[pl.ds(mine, rows)], send_sem=lens_sem.at[0], recv_sem=lens_sem.at[1],
         device_id={"ctx": mate}, device_id_type=MESH)
+    kv_slice = kv_out_ref.at[:, :, pl.ds(core * half_heads, half_heads)]
+    kv_store = pltpu.make_async_copy(kv_mine_buf, kv_slice, kv_sem.at[2])
     kv_send = pltpu.make_async_remote_copy(
-        src_ref=kv_send_buf, dst_ref=kv_out_ref.at[:, :, pl.ds(core * half_heads, half_heads)], send_sem=kv_sem.at[0], recv_sem=kv_sem.at[1],
+        src_ref=kv_send_buf, dst_ref=kv_slice, send_sem=kv_sem.at[0], recv_sem=kv_sem.at[1],
         device_id={"ctx": mate}, device_id_type=MESH)
 
     for layer in range(2):
         for copy in raw_loads(layer):
             copy.start()
-    for copy in suf_loads(0):
-        copy.start()
-
     for i in range(len(blocks)):
         for copy in qkv_copies(0, i):
             copy.start()
+        if i == 0:
+            for copy in suf_loads(0):
+                copy.start()
     for i in range(len(blocks)):
         wo_copy(0, i).start()
     for copy in suf_loads(1):
@@ -161,10 +164,12 @@
     key_ids = lax.broadcasted_iota(jnp.int32, (2 * PAD, 128), 1)
     key_slot = jnp.where(lax.rem(key_ids, 4) == 2 * core + row_ids // PAD, key_ids // 4, slots)[None]
 
-    def update_x(parity, j):
+    def await_part(parity, j):
         copy = part_send(parity, j)
         copy.wait_recv()
         copy.wait_send()
+
+    def update_x(parity, j):
         update = (own_buf[j] + recv_buf[parity, j]).astype(BF16)
         cols = slice(j * TILE, (j + 1) * TILE)
         x_buf[:, cols] = (x_buf[:, cols].astype(F32) + update.astype(F32)).astype(BF16)
@@ -194,6 +199,8 @@
             if i + 1 < len(blocks):
                 for copy in qkv_copies(layer, i + 1):
                     copy.wait()
+            for j in range(a, b):
+                await_part(parity_in, j)
             for j in range(a, b):
                 update_x(parity_in, j)
             r = slice(a * TILE, b * TILE)
@@ -229,16 +236,12 @@
                 kvn_buf[kv, h] = fresh
         for h in range(2):
             for kv in range(2):
-                kv_out_ref[layer, kv, core * half_heads + h] = kvn_buf[kv, h, pl.ds(mine, rows), :]
+                kv_mine_buf[layer, kv, h] = kvn_buf[kv, h, pl.ds(mine, rows), :]
                 kv_send_buf[layer, kv, h] = kvn_buf[kv, h, pl.ds(other, rows), :]
 
         for k in range(3):
             pre_remote(layer, k).wait_recv()
         suf_send(layer).wait()
-
-        @pl.when(layer == layers - 1)
-        def _():
-            kv_send.start()
 
         per_core = rows // CHUNK
 
@@ -259,7 +262,7 @@
             v_suf = suf_buf[slot, 1, pl.ds(part, CHUNK)]
             q_pairs = q3.astype(BF16).reshape(CHUNK // 2, 4 * PAD, head_dim)
             k_pairs = k_suf.reshape(CHUNK // 2, 256, head_dim)
-            suf_scores = unpair(lax.dot_general(q_pairs, k_pairs, (((2,), (2,)), ((0,), (0,))), preferred_element_type=F32)) * scale
+            suf_scores = unpair(lax.dot_general(q_pairs, k_pairs, (((2,), (2,)), ((0,), (0,))), preferred_element_type=F32))
             suf_scores = jnp.where(key_slot < lens_buf[pl.ds(first, CHUNK)], suf_scores, -jnp.inf)
             def spread(kv):
                 picked = [jnp.broadcast_to(kvn_buf[kv, h, pl.ds(first + b, 1), :], (PAD, head_dim)) for b in range(CHUNK) for h in range(2)]
@@ -267,20 +270,20 @@
 
             k_new = spread(0)
             v_new = spread(1)
-            new_scores = jnp.sum(q3 * k_new, axis=-1, keepdims=True) * scale
+            new_scores = jnp.sum(q3 * k_new, axis=-1, keepdims=True)
             suf_weights, new_weights, masses, pre_vals = [], [], [], []
             for h in range(2):
                 hs = slice(h * PAD, (h + 1) * PAD)
                 q_h = q3[:, hs, :].reshape(CHUNK * PAD, head_dim).astype(BF16)
                 k_pre = pre_buf[layer, 0, h].reshape(-1, head_dim)
                 v_pre = pre_buf[layer, 1, h].reshape(-1, head_dim)
-                scores = lax.dot_general(q_h, k_pre, (((1,), (1,)), ((), ())), preferred_element_type=F32) * scale
+                scores = lax.dot_general(q_h, k_pre, (((1,), (1,)), ((), ())), preferred_element_type=F32)
                 suf_h = suf_scores[:, hs, :].reshape(CHUNK * PAD, 128)
                 new_h = new_scores[:, hs, :].reshape(CHUNK * PAD, 1)
                 peak = jnp.maximum(jnp.maximum(scores.max(axis=-1, keepdims=True), suf_h.max(axis=-1, keepdims=True)), new_h)
-                pre_w = jnp.exp(scores - peak)
-                suf_w = jnp.exp(suf_h - peak)
-                new_w = jnp.exp(new_h - peak)
+                pre_w = jnp.exp2((scores - peak) * (scale * LOG2E))
+                suf_w = jnp.exp2((suf_h - peak) * (scale * LOG2E))
+                new_w = jnp.exp2((new_h - peak) * (scale * LOG2E))
                 masses.append(pre_w.sum(axis=-1, keepdims=True) + suf_w.sum(axis=-1, keepdims=True) + new_w)
                 pre_vals.append(jnp.dot(pre_w.astype(BF16), v_pre, preferred_element_type=F32))
                 suf_weights.append(suf_w.reshape(CHUNK, PAD, 128))
@@ -304,7 +307,14 @@
             return carry
 
         lax.fori_loop(0, 2 * per_core // CHUNKS_PER_TRIP, attend_trip, 0)
+
+        @pl.when(layer == layers - 1)
+        def _():
+            kv_store.start()
+            kv_send.start()
+
         wo_copy(layer, 0).wait()
+        wo_copy(layer, 1).wait()
 
         for h in range(2):
             for g in range(group):
@@ -312,7 +322,7 @@
                 att_buf[:, col:col + head_dim] = o_buf[pl.ds(h * PAD + g, both, stride=2 * PAD), :].astype(BF16)
 
         for i, (a, b) in enumerate(blocks):
-            if i + 1 < len(blocks):
+            if 0 < i < len(blocks) - 1:
                 wo_copy(layer, i + 1).wait()
             product = jnp.dot(att_buf[...], wo_buf[:, a * TILE:b * TILE], preferred_element_type=F32)
             for j in range(a, b):
@@ -329,21 +339,25 @@
 
     lax.fori_loop(0, layers, layer_body, 0)
     for j in range(tiles):
+        await_part((layers - 1) % 2, j)
+    for j in range(tiles):
         update_x((layers - 1) % 2, j)
         out_ref[:, j * TILE:(j + 1) * TILE] = x_buf[pl.ds(mine, rows), j * TILE:(j + 1) * TILE]
+    kv_store.wait()
     kv_send.wait()
 
 
-def cache_kernel(lens_ref, new_ref, k_ref, v_ref, k_out_ref, v_out_ref, buf, new_buf, in_sem, out_sem, new_sem):
+def cache_kernel(lens_ref, new_ref, hidden_ref, k_ref, v_ref, hidden_out_ref, k_out_ref, v_out_ref,
+                 buf, new_buf, hidden_buf, in_sem, out_sem, new_sem, hidden_sem):
     layers, rows, _, heads, _ = k_ref.shape
     ahead = RING // 2
 
     def loads(layer):
         slot = lax.rem(layer, RING)
         return (
+            pltpu.make_async_copy(new_ref.at[layer], new_buf.at[slot], new_sem.at[slot]),
             pltpu.make_async_copy(k_ref.at[layer], buf.at[slot, 0], in_sem.at[slot, 0]),
             pltpu.make_async_copy(v_ref.at[layer], buf.at[slot, 1], in_sem.at[slot, 1]),
-            pltpu.make_async_copy(new_ref.at[layer], new_buf.at[slot], new_sem.at[slot]),
         )
 
     def stores(layer):
@@ -356,6 +370,9 @@
     for layer in range(ahead):
         for copy in loads(layer):
             copy.start()
+    hidden_load = pltpu.make_async_copy(hidden_ref, hidden_buf, hidden_sem.at[0])
+    hidden_store = pltpu.make_async_copy(hidden_buf, hidden_out_ref, hidden_sem.at[1])
+    hidden_load.start()
 
     def step(layer, carry):
         slot = lax.rem(layer, RING)
@@ -370,19 +387,22 @@
             for copy in loads(layer + ahead):
                 copy.start()
 
-        for copy in loads(layer):
-            copy.wait()
-        for b in range(rows):
-            for kv in range(2):
+        arrivals = loads(layer)
+        arrivals[0].wait()
+        for kv in range(2):
+            arrivals[1 + kv].wait()
+            for b in range(rows):
                 buf[slot, kv, b, lens_ref[b]] = new_buf[slot, kv, pl.ds(b, heads, stride=rows), :].astype(BF16)
-        for copy in stores(layer):
-            copy.start()
+            stores(layer)[kv].start()
         return carry
 
     lax.fori_loop(0, layers, step, 0)
+    hidden_load.wait()
+    hidden_store.start()
     for layer in range(layers - ahead, layers):
         for copy in stores(layer):
             copy.wait()
+    hidden_store.wait()
 
 
 def solution(mesh):
@@ -420,7 +440,7 @@
             out_shape=(jax.ShapeDtypeStruct((rows, model_dim), BF16),
                        jax.ShapeDtypeStruct((layers, 2, kv_heads, rows, head_dim), F32)),
             in_specs=[vmem_spec, vmem_spec] + [any_spec] * 8,
-            out_specs=(vmem_spec, vmem_spec),
+            out_specs=(vmem_spec, any_spec),
             scratch_shapes=[
                 pltpu.VMEM((model_dim, q_width), BF16),
                 pltpu.VMEM((model_dim, kv_width), BF16),
@@ -441,26 +461,28 @@
                 pltpu.VMEM((both, q_width), BF16),
                 pltpu.VMEM((both, 2 * PAD, 128), jnp.int32),
                 pltpu.VMEM((layers, 2, half_heads, rows, head_dim), F32),
+                pltpu.VMEM((layers, 2, half_heads, rows, head_dim), F32),
                 dma((4, -(-tiles // BLOCK))), dma((3, 2)), dma((2,)), dma((2,)), dma((2, 2)), dma((layers, 3)), dma((layers, 3)),
-                dma((tiles,)), dma((2, tiles)), dma((2,)), dma((2,)),
+                dma((tiles,)), dma((2, tiles)), dma((2,)), dma((3,)),
             ],
             compiler_params=pltpu.CompilerParams(collective_id=0, has_side_effects=True, vmem_limit_bytes=66_000_000),
             name="decode_layers",
         )(seq_lens.reshape(1, rows), hidden, w_query, w_key, w_value, w_out, k_pre, v_pre, k_flat, v_flat)
 
-        k_out, v_out = pl.pallas_call(
+        hidden_out, k_out, v_out = pl.pallas_call(
             cache_kernel,
-            out_shape=(jax.ShapeDtypeStruct(k_suffix.shape, BF16), jax.ShapeDtypeStruct(v_suffix.shape, BF16)),
-            in_specs=[smem_spec] + [any_spec] * 3,
-            out_specs=(any_spec, any_spec),
+            out_shape=(jax.ShapeDtypeStruct(hidden.shape, BF16), jax.ShapeDtypeStruct(k_suffix.shape, BF16), jax.ShapeDtypeStruct(v_suffix.shape, BF16)),
+            in_specs=[smem_spec] + [any_spec] * 4,
+            out_specs=(any_spec, any_spec, any_spec),
             scratch_shapes=[
                 pltpu.VMEM((RING, 2) + k_suffix.shape[1:], BF16),
                 pltpu.VMEM((RING, 2, kv_heads * rows, head_dim), F32),
-                dma((RING, 2)), dma((RING, 2)), dma((RING,)),
+                pltpu.VMEM(hidden.shape, BF16),
+                dma((RING, 2)), dma((RING, 2)), dma((RING,)), dma((2,)),
             ],
             compiler_params=pltpu.CompilerParams(vmem_limit_bytes=60_000_000),
             name="write_caches",
-        )(seq_lens, kv_new.reshape(layers, 2, kv_heads * rows, head_dim), k_suffix, v_suffix)
+        )(seq_lens, kv_new.reshape(layers, 2, kv_heads * rows, head_dim), hidden_out, k_suffix, v_suffix)
         return hidden_out, k_out, v_out
 
     return jax.shard_map(local_step, mesh=mesh, in_specs=(row_spec, lens_spec, whole_spec, whole_spec, whole_spec, whole_spec, prefix_spec, prefix_spec, cache_spec, cache_spec), out_specs=(row_spec, cache_spec, cache_spec), check_vma=False)

time: 194 us -> 190 us (0.979)
  Pallas kernels: 192 us -> 189 us
    pallas_call x1, Pallas kernels: 168 us -> 165 us  [local_step(): pl.pallas_call(functools.partial(decode_kernel, (layers, rows, group, hea...]
where the time goes in v4:
time: 190 us
  Pallas kernels  189 us (99%)
    pallas_call x1, Pallas kernels, local_step(): pl.pallas_call(functools.partial(decode_kernel, (layers, rows, group, hea...  165 us
    pallas_call x1, Pallas kernels, local_step(): pl.pallas_call(cache_kernel, out_shape=(jax.ShapeDtypeStruct(hidden.shape...  24 us

profile of v4, /device:TPU:0, one launch (start us, length us, event | category | flops | bytes accessed | tf_op | source)
XLA Modules:
  0.0 189.5 jit_solution(8832029874510722935)
XLA Ops:
  0.6 164.8 %decode_layers.1 = (bf16[32,3584]{1,0:T(8,128)(2,1)}, f32[16,2,4,32,128]{4,3,2,1,0:T(8,128)}) custom-call(s32[1,32]{1,0:T(1,128)} %bitcast.11, bf16[32,3584]{1,0:T(8,128)(2,1)} %hidden_ref.1, bf16[16,3584,3584]{2,1,0:T(8,128)(2,1)} %wq_ref.1, bf16[16,3584,512]{2,1,0:T(8,128)(2,1)} %wk_ref.1, bf16[16,3584,512]{2,1,0:T(8,128)(2,1)} %wv_ref.1, ...), custom_call_target="tpu_custom_call" | custom-call | tf_op jit(solution)/shard_map/decode_layers/pallas_call | solution.py:438
  165.5 24.0 %write_caches.1 = (bf16[32,3584]{1,0:T(8,128)(2,1)}, bf16[16,32,32,4,128]{4,3,2,1,0:T(4,128)(2,1)}, bf16[16,32,32,4,128]{4,3,2,1,0:T(4,128)(2,1)}) custom-call(s32[32]{0:T(128)} %lens_ref.1, f32[16,2,128,128]{3,2,1,0:T(8,128)} %bitcast.10, bf16[32,3584]{1,0:T(8,128)(2,1)} %get-tuple-element.6.hidden_ref, bf16[16,32,32,4,128]{4,3,2,1,0:T(4,128)(2,1)} %k_ref.1, ...), custom_call_target="tpu_custom_call" | custom-call | tf_op jit(solution)/shard_map/write_caches/pallas_call | solution.py:472

commit v5 on v4

--- a/solution.py
+++ b/solution.py
@@ -30,7 +30,7 @@
     tiles = own_buf.shape[0]
     q_width = wq_buf.shape[1]
     kv_width = wk_buf.shape[1]
-    blocks = [(a, min(a + BLOCK, tiles)) for a in range(0, tiles, BLOCK)]
+    blocks = [(i * BLOCK, (i + 1) * BLOCK if i < tiles // BLOCK - 1 else tiles) for i in range(tiles // BLOCK)]
     both = 2 * rows
     me = lax.axis_index("ctx")
     core = lax.rem(me, 2)
@@ -229,7 +229,7 @@
         for h in range(2):
             for g in range(group):
                 col = (h * group + g) * head_dim
-                q_buf[pl.ds(h * PAD + g, both, stride=2 * PAD), :] = acc_buf[:, col:col + head_dim].astype(BF16).astype(F32)
+                q_buf[h, pl.ds(g, both, stride=PAD), :] = acc_buf[:, col:col + head_dim].astype(BF16).astype(F32)
             for kv in range(2):
                 col = q_width + kv * kv_width + h * head_dim
                 fresh = acc_buf[:, col:col + head_dim].astype(BF16).astype(F32)
@@ -255,9 +255,9 @@
             part = pl.multiple_of(lax.rem(i, per_core) * CHUNK, CHUNK)
             first = pl.multiple_of(lax.rem(core + away, 2) * rows + part, CHUNK)
             slot = (1 - away) * lax.rem(layer, 3) + away * (3 + lax.rem(layer, 2))
-            chunk_rows = pl.ds(pl.multiple_of(first * 2 * PAD, CHUNK * 2 * PAD), CHUNK * 2 * PAD)
-            q = q_buf[chunk_rows, :]
-            q3 = q.reshape(CHUNK, 2 * PAD, head_dim)
+            chunk_rows = pl.ds(pl.multiple_of(first * PAD, CHUNK * PAD), CHUNK * PAD)
+            q_heads = [q_buf[h, chunk_rows, :] for h in range(2)]
+            q3 = jnp.concatenate([q.reshape(CHUNK, PAD, head_dim) for q in q_heads], axis=1)
             k_suf = suf_buf[slot, 0, pl.ds(part, CHUNK)]
             v_suf = suf_buf[slot, 1, pl.ds(part, CHUNK)]
             q_pairs = q3.astype(BF16).reshape(CHUNK // 2, 4 * PAD, head_dim)
@@ -274,7 +274,7 @@
             suf_weights, new_weights, masses, pre_vals = [], [], [], []
             for h in range(2):
                 hs = slice(h * PAD, (h + 1) * PAD)
-                q_h = q3[:, hs, :].reshape(CHUNK * PAD, head_dim).astype(BF16)
+                q_h = q_heads[h].astype(BF16)
                 k_pre = pre_buf[layer, 0, h].reshape(-1, head_dim)
                 v_pre = pre_buf[layer, 1, h].reshape(-1, head_dim)
                 scores = lax.dot_general(q_h, k_pre, (((1,), (1,)), ((), ())), preferred_element_type=F32)
@@ -293,13 +293,11 @@
             v_pairs = jnp.concatenate([v_suf[:, 0], v_suf[:, 1]], axis=-1)
             suf_w = suf_w.reshape(CHUNK // 2, 4 * PAD, 128)
             suf_vals = unpair(lax.dot_general(suf_w, v_pairs, (((2,), (1,)), ((0,), (0,))), preferred_element_type=F32))
-            outs = []
             for h in range(2):
                 hs = slice(h * PAD, (h + 1) * PAD)
                 mixed = pre_vals[h] + suf_vals[:, hs, :].reshape(CHUNK * PAD, head_dim)
                 mixed = mixed + new_weights[h] * v_new[:, hs, :].reshape(CHUNK * PAD, head_dim)
-                outs.append((mixed / masses[h]).reshape(CHUNK, PAD, head_dim))
-            o_buf[chunk_rows, :] = jnp.concatenate(outs, axis=1).reshape(CHUNK * 2 * PAD, head_dim)
+                o_buf[h, chunk_rows, :] = mixed / masses[h]
 
         def attend_trip(trip, carry):
             for i in range(CHUNKS_PER_TRIP):
@@ -319,7 +317,7 @@
         for h in range(2):
             for g in range(group):
                 col = (h * group + g) * head_dim
-                att_buf[:, col:col + head_dim] = o_buf[pl.ds(h * PAD + g, both, stride=2 * PAD), :].astype(BF16)
+                att_buf[:, col:col + head_dim] = o_buf[h, pl.ds(g, both, stride=PAD), :].astype(BF16)
 
         for i, (a, b) in enumerate(blocks):
             if 0 < i < len(blocks) - 1:
@@ -455,14 +453,14 @@
                 pltpu.VMEM((tiles, both, TILE), F32),
                 pltpu.VMEM((2, tiles, both, TILE), F32),
                 pltpu.VMEM((both, q_width + 2 * kv_width), F32),
-                pltpu.VMEM((both * 2 * PAD, head_dim), F32),
+                pltpu.VMEM((half_heads, both * PAD, head_dim), F32),
                 pltpu.VMEM((2, half_heads, both, head_dim), F32),
-                pltpu.VMEM((both * 2 * PAD, head_dim), F32),
+                pltpu.VMEM((half_heads, both * PAD, head_dim), F32),
                 pltpu.VMEM((both, q_width), BF16),
                 pltpu.VMEM((both, 2 * PAD, 128), jnp.int32),
                 pltpu.VMEM((layers, 2, half_heads, rows, head_dim), F32),
                 pltpu.VMEM((layers, 2, half_heads, rows, head_dim), F32),
-                dma((4, -(-tiles // BLOCK))), dma((3, 2)), dma((2,)), dma((2,)), dma((2, 2)), dma((layers, 3)), dma((layers, 3)),
+                dma((4, tiles // BLOCK)), dma((3, 2)), dma((2,)), dma((2,)), dma((2, 2)), dma((layers, 3)), dma((layers, 3)),
                 dma((tiles,)), dma((2, tiles)), dma((2,)), dma((3,)),
             ],
             compiler_params=pltpu.CompilerParams(collective_id=0, has_side_effects=True, vmem_limit_bytes=66_000_000),

time: 190 us -> 189 us (level)
  no operation moved by 1% of the time
where the time goes in v5:
time: 189 us
  Pallas kernels  188 us (99%)
    pallas_call x1, Pallas kernels, local_step(): pl.pallas_call(functools.partial(decode_kernel, (layers, rows, group, hea...  164 us
    pallas_call x1, Pallas kernels, local_step(): pl.pallas_call(cache_kernel, out_shape=(jax.ShapeDtypeStruct(hidden.shape...  24 us

profile of v5, /device:TPU:0, one launch (start us, length us, event | category | flops | bytes accessed | tf_op | source)
XLA Modules:
  0.0 189.1 jit_solution(5978404981601360782)
XLA Ops:
  0.6 164.4 %decode_layers.1 = (bf16[32,3584]{1,0:T(8,128)(2,1)}, f32[16,2,4,32,128]{4,3,2,1,0:T(8,128)}) custom-call(s32[1,32]{1,0:T(1,128)} %bitcast.11, bf16[32,3584]{1,0:T(8,128)(2,1)} %hidden_ref.1, bf16[16,3584,3584]{2,1,0:T(8,128)(2,1)} %wq_ref.1, bf16[16,3584,512]{2,1,0:T(8,128)(2,1)} %wk_ref.1, bf16[16,3584,512]{2,1,0:T(8,128)(2,1)} %wv_ref.1, ...), custom_call_target="tpu_custom_call" | custom-call | tf_op jit(solution)/shard_map/decode_layers/pallas_call | solution.py:436
  165.0 24.0 %write_caches.1 = (bf16[32,3584]{1,0:T(8,128)(2,1)}, bf16[16,32,32,4,128]{4,3,2,1,0:T(4,128)(2,1)}, bf16[16,32,32,4,128]{4,3,2,1,0:T(4,128)(2,1)}) custom-call(s32[32]{0:T(128)} %lens_ref.1, f32[16,2,128,128]{3,2,1,0:T(8,128)} %bitcast.10, bf16[32,3584]{1,0:T(8,128)(2,1)} %get-tuple-element.6.hidden_ref, bf16[16,32,32,4,128]{4,3,2,1,0:T(4,128)(2,1)} %k_ref.1, ...), custom_call_target="tpu_custom_call" | custom-call | tf_op jit(solution)/shard_map/write_caches/pallas_call | solution.py:470

commit v6 on v5

--- a/solution.py
+++ b/solution.py
@@ -21,9 +21,9 @@
 
 def decode_kernel(dims, lens_ref, hidden_ref, wq_ref, wk_ref, wv_ref, wo_ref, kpre_ref, vpre_ref, ksuf_ref, vsuf_ref,
                   out_ref, kv_out_ref,
-                  wq_buf, wk_buf, wv_buf, wo_buf, pre_buf, raw_buf, wide_buf, split_buf, suf_buf, x_buf, own_buf, recv_buf, acc_buf,
+                  wq_buf, wk_buf, wv_buf, wo_first_buf, wo_buf, pre_buf, raw_buf, wide_buf, split_buf, suf_buf, x_buf, own_buf, recv_buf, acc_buf,
                   q_buf, kvn_buf, o_buf, att_buf, lens_buf, kv_mine_buf, kv_send_buf,
-                  w_sem, suf_load_sem, suf_send_sem, suf_recv_sem, raw_sem, pre_send_sem, pre_recv_sem,
+                  w_sem, wo_first_sem, suf_load_sem, suf_send_sem, suf_recv_sem, raw_sem, pre_send_sem, pre_recv_sem,
                   part_send_sem, part_recv_sem, lens_sem, kv_sem):
     layers, rows, group, head_dim, slots = dims
     half_heads = 2
@@ -56,8 +56,10 @@
 
     def wo_copy(layer, i):
         a, b = blocks[i]
-        cols = pl.ds(a * TILE, (b - a) * TILE)
-        return pltpu.make_async_copy(wo_ref.at[layer, pl.ds(q_col, q_width), cols], wo_buf.at[:, cols], w_sem.at[3, i])
+        src = wo_ref.at[layer, pl.ds(q_col, q_width), pl.ds(a * TILE, (b - a) * TILE)]
+        if i == 0:
+            return pltpu.make_async_copy(src, wo_first_buf.at[lax.rem(layer, 2)], wo_first_sem.at[lax.rem(layer, 2)])
+        return pltpu.make_async_copy(src, wo_buf.at[:, pl.ds((a - BLOCK) * TILE, (b - a) * TILE)], w_sem.at[3, i])
 
     def suf_loads(layer):
         slot = lax.rem(layer, 3)
@@ -225,6 +227,10 @@
                 def _():
                     for k in range(3):
                         pre_remote(layer + 2, k).start()
+
+        @pl.when(layer < layers - 1)
+        def _():
+            wo_copy(layer + 1, 0).start()
 
         for h in range(2):
             for g in range(group):
@@ -322,13 +328,15 @@
         for i, (a, b) in enumerate(blocks):
             if 0 < i < len(blocks) - 1:
                 wo_copy(layer, i + 1).wait()
-            product = jnp.dot(att_buf[...], wo_buf[:, a * TILE:b * TILE], preferred_element_type=F32)
+            weights = wo_first_buf[lax.rem(layer, 2)] if i == 0 else wo_buf[:, (a - BLOCK) * TILE:(b - BLOCK) * TILE]
+            product = jnp.dot(att_buf[...], weights, preferred_element_type=F32)
             for j in range(a, b):
                 own_buf[j] = product[:, (j - a) * TILE:(j - a + 1) * TILE]
 
-            @pl.when(layer < layers - 1)
-            def _():
-                wo_copy(layer + 1, i).start()
+            if i > 0:
+                @pl.when(layer < layers - 1)
+                def _():
+                    wo_copy(layer + 1, i).start()
 
             for j in range(a, b):
                 part_send(parity_out, j).start()
@@ -443,7 +451,8 @@
                 pltpu.VMEM((model_dim, q_width), BF16),
                 pltpu.VMEM((model_dim, kv_width), BF16),
                 pltpu.VMEM((model_dim, kv_width), BF16),
-                pltpu.VMEM((q_width, model_dim), BF16),
+                pltpu.VMEM((2, q_width, BLOCK * TILE), BF16),
+                pltpu.VMEM((q_width, model_dim - BLOCK * TILE), BF16),
                 pltpu.VMEM((layers, 2, half_heads, 4, positions, head_dim), BF16),
                 pltpu.VMEM((2, 2, positions * kv_heads, head_dim), BF16),
                 pltpu.VMEM((2, positions * kv_heads, head_dim), F32),
@@ -460,7 +469,7 @@
                 pltpu.VMEM((both, 2 * PAD, 128), jnp.int32),
                 pltpu.VMEM((layers, 2, half_heads, rows, head_dim), F32),
                 pltpu.VMEM((layers, 2, half_heads, rows, head_dim), F32),
-                dma((4, tiles // BLOCK)), dma((3, 2)), dma((2,)), dma((2,)), dma((2, 2)), dma((layers, 3)), dma((layers, 3)),
+                dma((4, tiles // BLOCK)), dma((2,)), dma((3, 2)), dma((2,)), dma((2,)), dma((2, 2)), dma((layers, 3)), dma((layers, 3)),
                 dma((tiles,)), dma((2, tiles)), dma((2,)), dma((3,)),
             ],
             compiler_params=pltpu.CompilerParams(collective_id=0, has_side_effects=True, vmem_limit_bytes=66_000_000),

time: 189 us -> 189 us (level)
  no operation moved by 1% of the time
where the time goes in v6:
time: 189 us
  Pallas kernels  188 us (99%)
    pallas_call x1, Pallas kernels, local_step(): pl.pallas_call(functools.partial(decode_kernel, (layers, rows, group, hea...  164 us
    pallas_call x1, Pallas kernels, local_step(): pl.pallas_call(cache_kernel, out_shape=(jax.ShapeDtypeStruct(hidden.shape...  24 us

profile of v6, /device:TPU:0, one launch (start us, length us, event | category | flops | bytes accessed | tf_op | source)
XLA Modules:
  0.0 189.0 jit_solution(17348630156239638269)
XLA Ops:
  0.6 164.3 %decode_layers.1 = (bf16[32,3584]{1,0:T(8,128)(2,1)}, f32[16,2,4,32,128]{4,3,2,1,0:T(8,128)}) custom-call(s32[1,32]{1,0:T(1,128)} %bitcast.11, bf16[32,3584]{1,0:T(8,128)(2,1)} %hidden_ref.1, bf16[16,3584,3584]{2,1,0:T(8,128)(2,1)} %wq_ref.1, bf16[16,3584,512]{2,1,0:T(8,128)(2,1)} %wk_ref.1, bf16[16,3584,512]{2,1,0:T(8,128)(2,1)} %wv_ref.1, ...), custom_call_target="tpu_custom_call" | custom-call | tf_op jit(solution)/shard_map/decode_layers/pallas_call | solution.py:444
  164.9 24.0 %write_caches.1 = (bf16[32,3584]{1,0:T(8,128)(2,1)}, bf16[16,32,32,4,128]{4,3,2,1,0:T(4,128)(2,1)}, bf16[16,32,32,4,128]{4,3,2,1,0:T(4,128)(2,1)}) custom-call(s32[32]{0:T(128)} %lens_ref.1, f32[16,2,128,128]{3,2,1,0:T(8,128)} %bitcast.10, bf16[32,3584]{1,0:T(8,128)(2,1)} %get-tuple-element.6.hidden_ref, bf16[16,32,32,4,128]{4,3,2,1,0:T(4,128)(2,1)} %k_ref.1, ...), custom_call_target="tpu_custom_call" | custom-call | tf_op jit(solution)/shard_map/write_caches/pallas_call | solution.py:479

commit v7 on v6

--- a/solution.py
+++ b/solution.py
@@ -13,7 +13,7 @@
 TILE = 512
 CHUNK = 32
 PAD = 8
-RING = 8
+WRITE_LAG = 15
 BLOCK = 2
 LOG2E = 1.4426950408889634
 CHUNKS_PER_TRIP = 1
@@ -356,56 +356,48 @@
 def cache_kernel(lens_ref, new_ref, hidden_ref, k_ref, v_ref, hidden_out_ref, k_out_ref, v_out_ref,
                  buf, new_buf, hidden_buf, in_sem, out_sem, new_sem, hidden_sem):
     layers, rows, _, heads, _ = k_ref.shape
-    ahead = RING // 2
 
     def loads(layer):
-        slot = lax.rem(layer, RING)
         return (
-            pltpu.make_async_copy(new_ref.at[layer], new_buf.at[slot], new_sem.at[slot]),
-            pltpu.make_async_copy(k_ref.at[layer], buf.at[slot, 0], in_sem.at[slot, 0]),
-            pltpu.make_async_copy(v_ref.at[layer], buf.at[slot, 1], in_sem.at[slot, 1]),
+            pltpu.make_async_copy(new_ref.at[layer], new_buf.at[layer], new_sem.at[layer]),
+            pltpu.make_async_copy(k_ref.at[layer], buf.at[layer, 0], in_sem.at[layer, 0]),
+            pltpu.make_async_copy(v_ref.at[layer], buf.at[layer, 1], in_sem.at[layer, 1]),
         )
 
     def stores(layer):
-        slot = lax.rem(layer, RING)
         return (
-            pltpu.make_async_copy(buf.at[slot, 0], k_out_ref.at[layer], out_sem.at[slot, 0]),
-            pltpu.make_async_copy(buf.at[slot, 1], v_out_ref.at[layer], out_sem.at[slot, 1]),
+            pltpu.make_async_copy(buf.at[layer, 0], k_out_ref.at[layer], out_sem.at[layer, 0]),
+            pltpu.make_async_copy(buf.at[layer, 1], v_out_ref.at[layer], out_sem.at[layer, 1]),
         )
 
-    for layer in range(ahead):
-        for copy in loads(layer):
-            copy.start()
     hidden_load = pltpu.make_async_copy(hidden_ref, hidden_buf, hidden_sem.at[0])
     hidden_store = pltpu.make_async_copy(hidden_buf, hidden_out_ref, hidden_sem.at[1])
     hidden_load.start()
-
-    def step(layer, carry):
-        slot = lax.rem(layer, RING)
-
-        @pl.when(layer >= ahead)
+    for layer in range(layers):
+        for copy in loads(layer):
+            copy.start()
+
+    def patch(layer, carry):
+        for copy in loads(layer):
+            copy.wait()
+        for kv in range(2):
+            for b in range(rows):
+                buf[layer, kv, b, lens_ref[b]] = new_buf[layer, kv, pl.ds(b, heads, stride=rows), :].astype(BF16)
+
+        @pl.when(layer >= WRITE_LAG)
         def _():
-            for copy in stores(layer - ahead):
-                copy.wait()
-
-        @pl.when(layer < layers - ahead)
-        def _():
-            for copy in loads(layer + ahead):
+            for copy in stores(layer - WRITE_LAG):
                 copy.start()
 
-        arrivals = loads(layer)
-        arrivals[0].wait()
-        for kv in range(2):
-            arrivals[1 + kv].wait()
-            for b in range(rows):
-                buf[slot, kv, b, lens_ref[b]] = new_buf[slot, kv, pl.ds(b, heads, stride=rows), :].astype(BF16)
-            stores(layer)[kv].start()
         return carry
 
-    lax.fori_loop(0, layers, step, 0)
+    lax.fori_loop(0, layers, patch, 0)
+    for layer in range(layers - WRITE_LAG, layers):
+        for copy in stores(layer):
+            copy.start()
     hidden_load.wait()
     hidden_store.start()
-    for layer in range(layers - ahead, layers):
+    for layer in range(layers):
         for copy in stores(layer):
             copy.wait()
     hidden_store.wait()
@@ -482,10 +474,10 @@
             in_specs=[smem_spec] + [any_spec] * 4,
             out_specs=(any_spec, any_spec, any_spec),
             scratch_shapes=[
-                pltpu.VMEM((RING, 2) + k_suffix.shape[1:], BF16),
-                pltpu.VMEM((RING, 2, kv_heads * rows, head_dim), F32),
+                pltpu.VMEM((layers, 2) + k_suffix.shape[1:], BF16),
+                pltpu.VMEM((layers, 2, kv_heads * rows, head_dim), F32),
                 pltpu.VMEM(hidden.shape, BF16),
-                dma((RING, 2)), dma((RING, 2)), dma((RING,)), dma((2,)),
+                dma((layers, 2)), dma((layers, 2)), dma((layers,)), dma((2,)),
             ],
             compiler_params=pltpu.CompilerParams(vmem_limit_bytes=60_000_000),
             name="write_caches",

time: 189 us -> 189 us (level)
  no operation moved by 1% of the time
where the time goes in v7:
time: 189 us
  Pallas kernels  188 us (99%)
    pallas_call x1, Pallas kernels, local_step(): pl.pallas_call(functools.partial(decode_kernel, (layers, rows, group, hea...  164 us
    pallas_call x1, Pallas kernels, local_step(): pl.pallas_call(cache_kernel, out_shape=(jax.ShapeDtypeStruct(hidden.shape...  23.6 us

profile of v7, /device:TPU:0, one launch (start us, length us, event | category | flops | bytes accessed | tf_op | source)
XLA Modules:
  0.0 188.5 jit_solution(18198218166357195466)
XLA Ops:
  0.6 164.3 %decode_layers.1 = (bf16[32,3584]{1,0:T(8,128)(2,1)}, f32[16,2,4,32,128]{4,3,2,1,0:T(8,128)}) custom-call(s32[1,32]{1,0:T(1,128)} %bitcast.11, bf16[32,3584]{1,0:T(8,128)(2,1)} %hidden_ref.1, bf16[16,3584,3584]{2,1,0:T(8,128)(2,1)} %wq_ref.1, bf16[16,3584,512]{2,1,0:T(8,128)(2,1)} %wk_ref.1, bf16[16,3584,512]{2,1,0:T(8,128)(2,1)} %wv_ref.1, ...), custom_call_target="tpu_custom_call" | custom-call | tf_op jit(solution)/shard_map/decode_layers/pallas_call | solution.py:436
  164.9 23.6 %write_caches.1 = (bf16[32,3584]{1,0:T(8,128)(2,1)}, bf16[16,32,32,4,128]{4,3,2,1,0:T(4,128)(2,1)}, bf16[16,32,32,4,128]{4,3,2,1,0:T(4,128)(2,1)}) custom-call(s32[32]{0:T(128)} %lens_ref.1, f32[16,2,128,128]{3,2,1,0:T(8,128)} %bitcast.10, bf16[32,3584]{1,0:T(8,128)(2,1)} %get-tuple-element.6.hidden_ref, bf16[16,32,32,4,128]{4,3,2,1,0:T(4,128)(2,1)} %k_ref.1, ...), custom_call_target="tpu_custom_call" | custom-call | tf_op jit(solution)/shard_map/write_caches/pallas_call | solution.py:471

commit v8 on v7

--- a/solution.py
+++ b/solution.py
@@ -19,11 +19,11 @@
 CHUNKS_PER_TRIP = 1
 
 
-def decode_kernel(dims, lens_ref, hidden_ref, wq_ref, wk_ref, wv_ref, wo_ref, kpre_ref, vpre_ref, ksuf_ref, vsuf_ref,
+def decode_kernel(dims, lens_hbm, hidden_hbm, wq_ref, wk_ref, wv_ref, wo_ref, kpre_ref, vpre_ref, ksuf_ref, vsuf_ref,
                   out_ref, kv_out_ref,
-                  wq_buf, wk_buf, wv_buf, wo_first_buf, wo_buf, pre_buf, raw_buf, wide_buf, split_buf, suf_buf, x_buf, own_buf, recv_buf, acc_buf,
+                  lens_ref, hidden_ref, wq_buf, wk_buf, wv_buf, wo_first_buf, wo_buf, pre_buf, raw_buf, wide_buf, split_buf, suf_buf, x_buf, own_buf, recv_buf, acc_buf,
                   q_buf, kvn_buf, o_buf, att_buf, lens_buf, kv_mine_buf, kv_send_buf,
-                  w_sem, wo_first_sem, suf_load_sem, suf_send_sem, suf_recv_sem, raw_sem, pre_send_sem, pre_recv_sem,
+                  entry_sem, w_sem, wo_first_sem, suf_load_sem, suf_send_sem, suf_recv_sem, raw_sem, pre_send_sem, pre_recv_sem,
                   part_send_sem, part_recv_sem, lens_sem, kv_sem):
     layers, rows, group, head_dim, slots = dims
     half_heads = 2
@@ -116,6 +116,12 @@
         src_ref=kv_send_buf, dst_ref=kv_slice, send_sem=kv_sem.at[0], recv_sem=kv_sem.at[1],
         device_id={"ctx": mate}, device_id_type=MESH)
 
+    barrier = pltpu.get_barrier_semaphore()
+    for device, _ in peers:
+        pl.semaphore_signal(barrier, inc=1, device_id={"ctx": device}, device_id_type=MESH)
+    entry_copies = (pltpu.make_async_copy(hidden_hbm, hidden_ref, entry_sem.at[0]), pltpu.make_async_copy(lens_hbm, lens_ref, entry_sem.at[1]))
+    for copy in entry_copies:
+        copy.start()
     for layer in range(2):
         for copy in raw_loads(layer):
             copy.start()
@@ -131,6 +137,9 @@
         copy.start()
 
     x_buf[...] = jnp.zeros_like(x_buf)
+    q_buf[...] = jnp.zeros_like(q_buf)
+    for copy in entry_copies:
+        copy.wait()
     for j in range(tiles):
         own_buf[j] = jnp.zeros_like(own_buf[j])
         own_buf[j, pl.ds(mine, rows), :] = hidden_ref[:, j * TILE:(j + 1) * TILE].astype(F32)
@@ -140,15 +149,11 @@
     lens_wide = jnp.broadcast_to(lens_wide, (rows, 128)).astype(jnp.int32)
     for b in range(rows):
         lens_buf[mine + b] = jnp.broadcast_to(lens_wide[b:b + 1, :], (2 * PAD, 128))
-    q_buf[...] = jnp.zeros_like(q_buf)
     split_prefix(0)
     for copy in raw_loads(2):
         copy.start()
     split_prefix(1)
 
-    barrier = pltpu.get_barrier_semaphore()
-    for device, _ in peers:
-        pl.semaphore_signal(barrier, inc=1, device_id={"ctx": device}, device_id_type=MESH)
     pl.semaphore_wait(barrier, 3)
 
     for j in range(tiles):
@@ -242,8 +247,8 @@
                 kvn_buf[kv, h] = fresh
         for h in range(2):
             for kv in range(2):
-                kv_mine_buf[layer, kv, h] = kvn_buf[kv, h, pl.ds(mine, rows), :]
-                kv_send_buf[layer, kv, h] = kvn_buf[kv, h, pl.ds(other, rows), :]
+                kv_mine_buf[layer, kv, h] = kvn_buf[kv, h, pl.ds(mine, rows), :].astype(BF16)
+                kv_send_buf[layer, kv, h] = kvn_buf[kv, h, pl.ds(other, rows), :].astype(BF16)
 
         for k in range(3):
             pre_remote(layer, k).wait_recv()
@@ -353,8 +358,8 @@
     kv_send.wait()
 
 
-def cache_kernel(lens_ref, new_ref, hidden_ref, k_ref, v_ref, hidden_out_ref, k_out_ref, v_out_ref,
-                 buf, new_buf, hidden_buf, in_sem, out_sem, new_sem, hidden_sem):
+def cache_kernel(lens_hbm, new_ref, hidden_ref, k_ref, v_ref, hidden_out_ref, k_out_ref, v_out_ref,
+                 buf, new_buf, wide_buf, lens_ref, hidden_buf, in_sem, out_sem, new_sem, hidden_sem):
     layers, rows, _, heads, _ = k_ref.shape
 
     def loads(layer):
@@ -372,17 +377,22 @@
 
     hidden_load = pltpu.make_async_copy(hidden_ref, hidden_buf, hidden_sem.at[0])
     hidden_store = pltpu.make_async_copy(hidden_buf, hidden_out_ref, hidden_sem.at[1])
-    hidden_load.start()
+    lens_load = pltpu.make_async_copy(lens_hbm, lens_ref, hidden_sem.at[2])
     for layer in range(layers):
         for copy in loads(layer):
             copy.start()
+        if layer == 0:
+            lens_load.start()
+            hidden_load.start()
+    lens_load.wait()
 
     def patch(layer, carry):
         for copy in loads(layer):
             copy.wait()
         for kv in range(2):
+            wide_buf[kv] = new_buf[layer, kv].astype(F32)
             for b in range(rows):
-                buf[layer, kv, b, lens_ref[b]] = new_buf[layer, kv, pl.ds(b, heads, stride=rows), :].astype(BF16)
+                buf[layer, kv, b, lens_ref[b]] = wide_buf[kv, pl.ds(b, heads, stride=rows), :].astype(BF16)
 
         @pl.when(layer >= WRITE_LAG)
         def _():
@@ -430,16 +440,17 @@
         v_pre = v_prefix.reshape(layers, positions * kv_heads, head_dim)
 
         any_spec = pl.BlockSpec(memory_space=pl.ANY)
-        smem_spec = pl.BlockSpec(memory_space=pltpu.SMEM)
         vmem_spec = pl.BlockSpec(memory_space=pltpu.VMEM)
         dma = pltpu.SemaphoreType.DMA
         hidden_out, kv_new = pl.pallas_call(
             functools.partial(decode_kernel, (layers, rows, group, head_dim, slots)),
             out_shape=(jax.ShapeDtypeStruct((rows, model_dim), BF16),
-                       jax.ShapeDtypeStruct((layers, 2, kv_heads, rows, head_dim), F32)),
-            in_specs=[vmem_spec, vmem_spec] + [any_spec] * 8,
+                       jax.ShapeDtypeStruct((layers, 2, kv_heads, rows, head_dim), BF16)),
+            in_specs=[any_spec] * 10,
             out_specs=(vmem_spec, any_spec),
             scratch_shapes=[
+                pltpu.VMEM((1, rows), jnp.int32),
+                pltpu.VMEM(hidden.shape, BF16),
                 pltpu.VMEM((model_dim, q_width), BF16),
                 pltpu.VMEM((model_dim, kv_width), BF16),
                 pltpu.VMEM((model_dim, kv_width), BF16),
@@ -459,9 +470,9 @@
                 pltpu.VMEM((half_heads, both * PAD, head_dim), F32),
                 pltpu.VMEM((both, q_width), BF16),
                 pltpu.VMEM((both, 2 * PAD, 128), jnp.int32),
-                pltpu.VMEM((layers, 2, half_heads, rows, head_dim), F32),
-                pltpu.VMEM((layers, 2, half_heads, rows, head_dim), F32),
-                dma((4, tiles // BLOCK)), dma((2,)), dma((3, 2)), dma((2,)), dma((2,)), dma((2, 2)), dma((layers, 3)), dma((layers, 3)),
+                pltpu.VMEM((layers, 2, half_heads, rows, head_dim), BF16),
+                pltpu.VMEM((layers, 2, half_heads, rows, head_dim), BF16),
+                dma((2,)), dma((4, tiles // BLOCK)), dma((2,)), dma((3, 2)), dma((2,)), dma((2,)), dma((2, 2)), dma((layers, 3)), dma((layers, 3)),
                 dma((tiles,)), dma((2, tiles)), dma((2,)), dma((3,)),
             ],
             compiler_params=pltpu.CompilerParams(collective_id=0, has_side_effects=True, vmem_limit_bytes=66_000_000),
@@ -471,13 +482,15 @@
         hidden_out, k_out, v_out = pl.pallas_call(
             cache_kernel,
             out_shape=(jax.ShapeDtypeStruct(hidden.shape, BF16), jax.ShapeDtypeStruct(k_suffix.shape, BF16), jax.ShapeDtypeStruct(v_suffix.shape, BF16)),
-            in_specs=[smem_spec] + [any_spec] * 4,
+            in_specs=[any_spec] * 5,
             out_specs=(any_spec, any_spec, any_spec),
             scratch_shapes=[
                 pltpu.VMEM((layers, 2) + k_suffix.shape[1:], BF16),
-                pltpu.VMEM((layers, 2, kv_heads * rows, head_dim), F32),
+                pltpu.VMEM((layers, 2, kv_heads * rows, head_dim), BF16),
+                pltpu.VMEM((2, kv_heads * rows, head_dim), F32),
+                pltpu.SMEM(seq_lens.shape, jnp.int32),
                 pltpu.VMEM(hidden.shape, BF16),
-                dma((layers, 2)), dma((layers, 2)), dma((layers,)), dma((2,)),
+                dma((layers, 2)), dma((layers, 2)), dma((layers,)), dma((3,)),
             ],
             compiler_params=pltpu.CompilerParams(vmem_limit_bytes=60_000_000),
             name="write_caches",

time: 189 us -> 186 us (0.984)
  Pallas kernels: 188 us -> 185 us
    pallas_call x1, Pallas kernels: 164 us -> 162 us  [local_step(): pl.pallas_call(functools.partial(decode_kernel, (layers, rows, group, hea...]
where the time goes in v8:
time: 186 us
  Pallas kernels  185 us (99%)
    pallas_call x1, Pallas kernels, local_step(): pl.pallas_call(functools.partial(decode_kernel, (layers, rows, group, hea...  162 us
    pallas_call x1, Pallas kernels, local_step(): pl.pallas_call(cache_kernel, out_shape=(jax.ShapeDtypeStruct(hidden.shape...  22.7 us

profile of v8, /device:TPU:0, one launch (start us, length us, event | category | flops | bytes accessed | tf_op | source)
XLA Modules:
  0.0 185.5 jit_solution(15468473280576094342)
XLA Ops:
  0.6 162.2 %decode_layers.1 = (bf16[32,3584]{1,0:T(8,128)(2,1)}, bf16[16,2,4,32,128]{4,3,2,1,0:T(8,128)(2,1)}) custom-call(s32[1,32]{1,0:T(1,128)} %bitcast.11, bf16[32,3584]{1,0:T(8,128)(2,1)} %hidden_hbm.1, bf16[16,3584,3584]{2,1,0:T(8,128)(2,1)} %wq_ref.1, bf16[16,3584,512]{2,1,0:T(8,128)(2,1)} %wk_ref.1, bf16[16,3584,512]{2,1,0:T(8,128)(2,1)} %wv_ref.1, ...), custom_call_target="tpu_custom_call" | custom-call | tf_op jit(solution)/shard_map/decode_layers/pallas_call | solution.py:445
  162.9 22.7 %write_caches.1 = (bf16[32,3584]{1,0:T(8,128)(2,1)}, bf16[16,32,32,4,128]{4,3,2,1,0:T(4,128)(2,1)}, bf16[16,32,32,4,128]{4,3,2,1,0:T(4,128)(2,1)}) custom-call(s32[32]{0:T(128)} %lens_hbm.1, bf16[16,2,128,128]{3,2,1,0:T(8,128)(2,1)} %bitcast.10, bf16[32,3584]{1,0:T(8,128)(2,1)} %get-tuple-element.6.hidden_ref, bf16[16,32,32,4,128]{4,3,2,1,0:T(4,128)(2,1)} %k_ref.1, ...), custom_call_target="tpu_custom_call" | custom-call | tf_op jit(solution)/shard_map/write_caches/pallas_call | solution.py:482

commit v9 on v8

--- a/solution.py
+++ b/solution.py
@@ -13,7 +13,7 @@
 TILE = 512
 CHUNK = 32
 PAD = 8
-WRITE_LAG = 15
+WRITE_LAG = 8
 BLOCK = 2
 LOG2E = 1.4426950408889634
 CHUNKS_PER_TRIP = 1
@@ -349,11 +349,13 @@
         return carry
 
     lax.fori_loop(0, layers, layer_body, 0)
+    home = pl.ds(mine, rows)
     for j in range(tiles):
-        await_part((layers - 1) % 2, j)
-    for j in range(tiles):
-        update_x((layers - 1) % 2, j)
-        out_ref[:, j * TILE:(j + 1) * TILE] = x_buf[pl.ds(mine, rows), j * TILE:(j + 1) * TILE]
+        parity = (layers - 1) % 2
+        await_part(parity, j)
+        cols = slice(j * TILE, (j + 1) * TILE)
+        update = (own_buf[j, home, :] + recv_buf[parity, j, home, :]).astype(BF16)
+        out_ref[:, cols] = (x_buf[home, cols].astype(F32) + update.astype(F32)).astype(BF16)
     kv_store.wait()
     kv_send.wait()
 

time: 186 us -> 185 us (level)
  no operation moved by 1% of the time
where the time goes in v9:
time: 185 us
  Pallas kernels  184 us (99%)
    pallas_call x1, Pallas kernels, local_step(): pl.pallas_call(functools.partial(decode_kernel, (layers, rows, group, hea...  162 us
    pallas_call x1, Pallas kernels, local_step(): pl.pallas_call(cache_kernel, out_shape=(jax.ShapeDtypeStruct(hidden.shape...  22.2 us

profile of v9, /device:TPU:0, one launch (start us, length us, event | category | flops | bytes accessed | tf_op | source)
XLA Modules:
  0.0 184.9 jit_solution(8161586830396355367)
XLA Ops:
  0.6 162.0 %decode_layers.1 = (bf16[32,3584]{1,0:T(8,128)(2,1)}, bf16[16,2,4,32,128]{4,3,2,1,0:T(8,128)(2,1)}) custom-call(s32[1,32]{1,0:T(1,128)} %bitcast.11, bf16[32,3584]{1,0:T(8,128)(2,1)} %hidden_hbm.1, bf16[16,3584,3584]{2,1,0:T(8,128)(2,1)} %wq_ref.1, bf16[16,3584,512]{2,1,0:T(8,128)(2,1)} %wk_ref.1, bf16[16,3584,512]{2,1,0:T(8,128)(2,1)} %wv_ref.1, ...), custom_call_target="tpu_custom_call" | custom-call | tf_op jit(solution)/shard_map/decode_layers/pallas_call | solution.py:447
  162.7 22.2 %write_caches.1 = (bf16[32,3584]{1,0:T(8,128)(2,1)}, bf16[16,32,32,4,128]{4,3,2,1,0:T(4,128)(2,1)}, bf16[16,32,32,4,128]{4,3,2,1,0:T(4,128)(2,1)}) custom-call(s32[32]{0:T(128)} %lens_hbm.1, bf16[16,2,128,128]{3,2,1,0:T(8,128)(2,1)} %bitcast.10, bf16[32,3584]{1,0:T(8,128)(2,1)} %get-tuple-element.6.hidden_ref, bf16[16,32,32,4,128]{4,3,2,1,0:T(4,128)(2,1)} %k_ref.1, ...), custom_call_target="tpu_custom_call" | custom-call | tf_op jit(solution)/shard_map/write_caches/pallas_call | solution.py:484
